TPU v7x, 256 devices: a whole 4x4x8 slice. The times are simulated.
256 devices in a mesh: block: 8 (over y, core), patch: 32 (over z, x).
Axes of the slice: x: 4, y: 4, z: 8, core: 2. Of those that a mesh axis runs over, the one named last changes fastest.
Arguments:
- samples_in: bfloat16 [16, 32, 2048, 128], P('block', None, 'patch'), may hold values from -6 to 6
- block_order: int32 [32, 16], P('patch'), may hold values from 0 to 15, each once within a row
- seam_link: int32 [32], P('patch'), may hold values from 0 to 1, as said below
- w_in: bfloat16 [16, 32, 256], P('block'), may hold values from -1.5 to 1.5
- w_mid: bfloat16 [16, 2, 256, 256], P('block'), may hold values from -0.5 to 0.5
- w_feat: bfloat16 [16, 256, 64], P('block'), may hold values from -0.375 to 0.375
- w_density: bfloat16 [16, 256], P('block'), may hold values from -0.375 to 0.375
- w_conv: bfloat16 [4, 3, 3, 64, 64], replicated, may hold values from -0.375 to 0.375
- w_color: bfloat16 [3, 64], replicated, may hold values from -0.75 to 0.75
Outputs:
- pixels: float32 [3, 128, 8192], P(None, 'block', 'patch')
Inputs may be any that keep to these rules, and one draw needn't show every extreme that they name: Each row of block_order names every one of the 16 blocks once, in the order in which that patch's rays pass them, nearest first. seam_link[p] is 1 where patch p + 1 continues patch p to the right in one image; the entry before last is always 1; the last entry is not read.
All inputs are finite; a program needn't handle non-finite values.
Results may differ from a plain program's by a relative error of at most 0.015.
Values may be sent and summed in bfloat16 or wider, within the bound.
A program may use at most 64 MiB of HBM per device.

v0:
```python
import jax
import jax.numpy as jnp
from jax import lax
from jax.sharding import PartitionSpec as P

ENC = 32
SAMP = 4


step_length = 0.03
highest = lax.Precision.HIGHEST


def in_order(pieces, dim):
    pieces = jnp.moveaxis(pieces, 0, dim)
    shape = pieces.shape
    return pieces.reshape(*shape[:dim], shape[dim] * shape[dim + 1], *shape[dim + 2 :])


def from_everyone(x, axis):
    copies = jnp.broadcast_to(x, (lax.axis_size(axis), *x.shape))
    return lax.all_to_all(copies, axis, split_axis=0, concat_axis=0, tiled=True)


def gather_directly(x, axis, dim):
    return in_order(from_everyone(x, axis), dim)


def split_up(x, dim, devices):
    before, after = (x.shape[:dim], x.shape[dim + 1 :])
    return jnp.moveaxis(x.reshape(*before, devices, -1, *after), dim, 0)


def sent_and_summed(x, axis, dim):
    devices = lax.axis_size(axis)
    pieces = lax.all_to_all(split_up(x, dim, devices), axis, 0, 0, tiled=True)
    return jnp.sum(pieces, axis=0)


def shifted(block, axis, distance):
    devices = range(lax.axis_size(axis))
    route = [(i - distance, i) for i in devices if i - distance in devices]
    return lax.ppermute(block, axis, route)


def padded_2(block, sides, width):
    for axis, dim in sides:
        count = lax.axis_size(axis)
        forward = [(i, i + 1) for i in range(count - 1)]
        backward = [(target, source) for source, target in forward]
        low = lax.ppermute(
            lax.slice_in_dim(block, block.shape[dim] - width, None, axis=dim), axis, forward
        )
        high = lax.ppermute(lax.slice_in_dim(block, 0, width, axis=dim), axis, backward)
        block = jnp.concatenate([low, block, high], axis=dim)
    return block


def block_field(samples, w_first, w_hidden, w_head, w_dens):
    count = samples.shape[0]
    flat = samples.reshape(count * SAMP, ENC)
    hidden = jax.nn.relu(jnp.dot(flat, w_first, preferred_element_type=jnp.float32)).astype(
        jnp.bfloat16
    )
    hidden = jax.nn.relu(jnp.dot(hidden, w_hidden[0], preferred_element_type=jnp.float32)).astype(
        jnp.bfloat16
    )
    hidden = jax.nn.relu(jnp.dot(hidden, w_hidden[1], preferred_element_type=jnp.float32)).astype(
        jnp.bfloat16
    )
    feature = lax.dot_general(
        w_head, hidden, (((0,), (1,)), ((), ())), preferred_element_type=jnp.float32
    )
    density = jax.nn.softplus(jnp.dot(hidden, w_dens, preferred_element_type=jnp.float32))
    optical = step_length * density.reshape(count, SAMP)
    earlier = jnp.cumsum(optical, axis=1) - optical
    weights = jnp.exp(-earlier) * -jnp.expm1(-optical)
    colour = jnp.sum(feature.reshape(feature.shape[0], count, SAMP) * weights[None], axis=2)
    return (jnp.sum(optical, axis=1), colour)


def ranks_of(order_row):
    blocks = order_row.shape[0]
    places = jnp.arange(blocks, dtype=jnp.int32)
    hits = (order_row[None, :] == places[:, None]).astype(jnp.int32)
    return jnp.sum(places[None, :] * hits, axis=1)


def enlarge(image):
    return jnp.repeat(jnp.repeat(image, 2, axis=1), 2, axis=2)


def conv_valid(padded, kernel):
    rows = padded.shape[1] - 2
    width = padded.shape[2] - 2
    result = jnp.zeros((kernel.shape[2], rows, width), jnp.float32)
    for down in range(3):
        for across in range(3):
            window = padded[:, down : down + rows, across : across + width]
            result = result + lax.dot_general(
                kernel[down, across],
                window,
                (((1,), (0,)), ((), ())),
                preferred_element_type=jnp.float32,
            )
    return result


def open_columns(padded, rim, left_open, right_open):
    width = padded.shape[2]
    column = jnp.arange(width, dtype=jnp.int32)
    scale = jnp.where(
        column < rim,
        left_open,
        jnp.where(column >= width - rim, right_open, jnp.ones_like(left_open)),
    )
    return padded * scale[None, None, :]


def open_rows(padded, rim, top_open, bottom_open):
    height = padded.shape[1]
    row_ids = jnp.arange(height, dtype=jnp.int32)
    scale = jnp.where(
        row_ids < rim,
        top_open,
        jnp.where(row_ids >= height - rim, bottom_open, jnp.ones_like(top_open)),
    )
    return padded * scale[None, :, None]


def body(samples_in, block_order, seam_link, w_in, w_mid, w_feat, w_density, w_conv, w_color):
    blk_dev = samples_in.shape[0]
    groups = lax.axis_size("block")
    rows_all = samples_in.shape[1]
    cols_here = samples_in.shape[2]
    ray_count = rows_all * cols_here
    rays = samples_in.reshape(blk_dev, ray_count, samples_in.shape[3])
    depth_list = []
    colour_list = []
    for member in range(blk_dev):
        depth_sum, colour = block_field(
            rays[member], w_in[member], w_mid[member], w_feat[member], w_density[member]
        )
        depth_list.append(depth_sum)
        colour_list.append(colour)
    depth_own = jnp.stack(depth_list)
    colour_own = jnp.stack(colour_list)
    rank = ranks_of(block_order[0])
    position = lax.axis_index("block")
    depth_all = gather_directly(depth_own, "block", 0)
    rank_own = lax.dynamic_slice_in_dim(rank, position * blk_dev, blk_dev)
    earlier = (rank[:, None] < rank_own[None, :]).astype(jnp.float32)
    prefix = jnp.dot(earlier.T, depth_all, precision=highest)
    partial_sum = jnp.sum(jnp.exp(-prefix)[:, None, :] * colour_own, axis=0)
    mixed = sent_and_summed(partial_sum, "block", 1)
    rows_dev = ray_count // groups // cols_here
    composite = mixed.astype(jnp.bfloat16).reshape(mixed.shape[0], rows_dev, cols_here)
    patch_count = lax.axis_size("patch")
    patch_place = lax.axis_index("patch")
    left_open = shifted(seam_link, "patch", 1).astype(jnp.bfloat16)[0]
    right_open = (seam_link[0] * (patch_place < patch_count - 1).astype(jnp.int32)).astype(
        jnp.bfloat16
    )
    top_open = (position > 0).astype(jnp.bfloat16)
    bottom_open = (position < groups - 1).astype(jnp.bfloat16)

    def rim_pair(image, first_kernel, second_kernel):
        padded = padded_2(image, (("block", 1), ("patch", 2)), 1)
        padded = open_columns(padded, 1, left_open, right_open)
        middle = jax.nn.relu(conv_valid(enlarge(padded), first_kernel)).astype(jnp.bfloat16)
        middle = open_rows(open_columns(middle, 1, left_open, right_open), 1, top_open, bottom_open)
        return conv_valid(middle, second_kernel)

    decoded = jax.nn.relu(rim_pair(composite, w_conv[0], w_conv[1])).astype(jnp.bfloat16)
    final = rim_pair(decoded, w_conv[2], w_conv[3])
    return lax.dot_general(
        w_color.astype(jnp.float32), final, (((1,), (0,)), ((), ())), precision=highest
    )


def solution(mesh):
    return jax.shard_map(
        body,
        mesh=mesh,
        in_specs=(
            P("block", None, "patch", None),
            P("patch", None),
            P("patch"),
            P("block", None, None),
            P("block", None, None, None),
            P("block", None, None),
            P("block", None),
            P(),
            P(),
        ),
        out_specs=P(None, "block", "patch"),
        check_vma=False,
    )
```

profile of v0, /device:TPU:111, one launch (start us, length us, event | category | flops | bytes accessed | tf_op | source)
XLA Modules:
  0.0 156.9 jit_solution(10887867667157977555)
XLA Ops:
  0.0 2.1 %fusion.103 = (bf16[1,32,64,128]{3,2,1,0:T(8,128)(2,1)S(1)}, bf16[1,32,64,128]{3,2,1,0:T(8,128)(2,1)}) fusion(bf16[2,32,64,128]{3,2,1,0:T(8,128)(2,1)} %param.9), kind=kLoop, calls=%fused_computation.198 | loop fusion | bytes 2097152 | tf_op jit(solution)/shard_map/slice | solution.py:142
  2.1 0.8 reshape_squeeze.6
  3.0 4.0 %fusion.2 = bf16[8192,256]{1,0:T(8,128)(2,1)} fusion(bf16[8192,32]{1,0:T(8,128)(2,1)S(1)} %reshape_squeeze.6, bf16[2,2,256,256]{3,2,1,0:T(8,128)(2,1)S(1)} %copy-done.8, bf16[2,32,256]{2,1,0:T(8,128)(2,1)S(1)} %copy-done.11), kind=kOutput, calls=%fused_computation.8 | convolution fusion | flops 1216348160 | bytes 6438912 | tf_op jit(solution)/shard_map/dot_general | solution.py:65
  7.0 3.4 %fusion.3 = bf16[8192,256]{1,0:T(8,128)(2,1)S(1)} fusion(bf16[8192,256]{1,0:T(8,128)(2,1)} %fusion.2, bf16[2,2,256,256]{3,2,1,0:T(8,128)(2,1)S(1)} %copy-done.8), kind=kOutput, calls=%fused_computation.9 | convolution fusion | flops 1077936128 | bytes 8519680 | tf_op jit(solution)/shard_map/dot_general | solution.py:68
  10.5 1.2 fusion.94
  11.7 0.8 copy-done.1
  12.4 1.1 mul.130
  13.5 2.7 %reshape_squeeze.7 = bf16[8192,32]{1,0:T(8,128)(2,1)S(1)} reshape(bf16[1,32,64,128]{3,2,1,0:T(8,128)(2,1)} %get-tuple-element.10) | data formatting | bytes 1048576 | tf_op jit(solution)/shard_map/reshape;squeeze | solution.py:61
  16.2 4.9 %fusion.4 = bf16[8192,256]{1,0:T(8,128)(2,1)} fusion(bf16[8192,32]{1,0:T(8,128)(2,1)S(1)} %reshape_squeeze.7, bf16[2,2,256,256]{3,2,1,0:T(8,128)(2,1)} %param.13, bf16[2,32,256]{2,1,0:T(8,128)(2,1)S(1)} %copy-done.11), kind=kOutput, calls=%fused_computation.10 | convolution fusion | flops 1216348160 | bytes 6438912 | tf_op jit(solution)/shard_map/dot_general | solution.py:65
  21.1 3.4 %fusion.5 = bf16[8192,256]{1,0:T(8,128)(2,1)S(1)} fusion(bf16[8192,256]{1,0:T(8,128)(2,1)} %fusion.4, bf16[2,2,256,256]{3,2,1,0:T(8,128)(2,1)} %param.13), kind=kOutput, calls=%fused_computation.11 | convolution fusion | flops 1077936128 | bytes 8519680 | tf_op jit(solution)/shard_map/dot_general | solution.py:68
  24.6 1.2 fusion.92
  25.8 0.8 copy-done.2
  26.6 1.1 mul.132
  27.7 0.6 reduce_window_sum.17
  28.3 1.6 %reduce_window_sum.18 = f32[2048,4]{1,0:T(8,128)} reduce-window(f32[2048,4]{1,0:T(8,128)S(1)} %mul.132, f32[]{:T(128)} %constant.27.clone.1), window={size=1x4 pad=0_0x3_0}, to_apply=%region_5.6 | reduce-window | flops 24576 | bytes 65540 | tf_op jit(solution)/shard_map/jit(cumsum)/reduce_window_sum | solution.py:76
  29.9 3.3 %fusion.101 = (f32[2048]{0:T(1024)S(1)}, f32[2048,4]{1,0:T(8,128)}, f32[2048,4]{1,0:T(8,128)}, f32[2048]{0:T(1024)S(1)}) fusion(f32[2048,4]{1,0:T(8,128)S(1)} %mul.130, f32[2048,4]{1,0:T(8,128)S(1)} %reduce_window_sum.17, f32[2048,4]{1,0:T(8,128)S(1)} %mul.132, f32[2048,4]{1,0:T(8,128)} %reduce_window_sum.18), kind=kLoop, calls=%fused_computation.196 | loop fusion | flops 94208 | bytes 212992 | tf_op jit(solution)/shard_map/reduce_sum | solution.py:79
  33.3 0.7 broadcast_in_dim.91
  34.0 5.2 %all-to-all-start = ((f32[8,2,2048]{2,1,0:T(2,128)}), f32[8,2,2048]{2,1,0:T(2,128)S(1)}, u32[]{:S(2)}, u32[]{:S(2)}) async-start(f32[8,2,2048]{2,1,0:T(2,128)} %broadcast_in_dim.91), calls=%async_computation | async-start | bytes 262144 | tf_op jit(solution)/shard_map/all_to_all | solution.py:22
  39.2 3.7 %convolution_bitcast_fusion.1 = f32[64,8192]{1,0:T(8,128)S(1)} fusion(bf16[8192,256]{1,0:T(8,128)(2,1)} %copy-done.1, bf16[2,256,64]{1,2,0:T(8,128)(2,1)S(1)} %copy-done.9), kind=kOutput, calls=%fused_computation.13 | convolution fusion | flops 268435456 | bytes 6324224 | tf_op jit(solution)/shard_map/dot_general | solution.py:71
  42.9 2.7 %convolution_bitcast_fusion = f32[64,8192]{1,0:T(8,128)} fusion(bf16[8192,256]{1,0:T(8,128)(2,1)S(1)} %copy-done.3, bf16[2,256,64]{1,2,0:T(8,128)(2,1)S(1)} %copy-done.9), kind=kOutput, calls=%fused_computation.12 | convolution fusion | flops 268435456 | bytes 6324224 | tf_op jit(solution)/shard_map/dot_general | solution.py:71
  45.6 2.7 %copy.131 = f32[64,8192]{0,1:T(8,128)} copy(f32[64,8192]{1,0:T(8,128)S(1)} %convolution_bitcast_fusion.1) | data formatting | bytes 4194304 | tf_op jit(solution)/shard_map/dot_general | solution.py:71
  48.4 3.9 %copy.132 = f32[64,8192]{0,1:T(8,128)} copy(f32[64,8192]{1,0:T(8,128)} %convolution_bitcast_fusion) | data formatting | bytes 4194304 | tf_op jit(solution)/shard_map/dot_general | solution.py:71
  52.2 12.5 %multiply_reduce_fusion.1 = f32[64,2048]{0,1:T(8,128)S(1)} fusion(f32[64,2048,4]{0,2,1:T(4,128)} %bitcast.278, f32[2048,4]{1,0:T(8,128)S(1)} %copy-done.6), kind=kLoop, calls=%fused_computation.15 | loop fusion | flops 917504 | bytes 2654208 | tf_op jit(solution)/shard_map/reduce_sum | solution.py:78
  64.7 11.2 %multiply_reduce_fusion = f32[64,2048]{0,1:T(8,128)S(1)} fusion(f32[64,2048,4]{0,2,1:T(4,128)S(1)} %bitcast.277, f32[2048,4]{1,0:T(8,128)S(1)} %copy-done.5), kind=kLoop, calls=%fused_computation.14 | loop fusion | flops 917504 | bytes 2654208 | tf_op jit(solution)/shard_map/reduce_sum | solution.py:78
  76.6 0.8 fusion.7
  77.4 1.1 copy.134
  78.5 4.8 %all-to-all-start.1 = ((f32[8,64,256]{2,1,0:T(8,128)}), f32[8,64,256]{2,1,0:T(8,128)S(1)}, u32[]{:S(2)}, u32[]{:S(2)}) async-start(f32[8,64,256]{2,1,0:T(8,128)} %copy.134), calls=%async_computation.1 | async-start | bytes 1048576 | tf_op jit(solution)/shard_map/all_to_all | solution.py:36
  83.3 4.7 %collective-permute-start.4 = (s32[1]{0:T(128)}, s32[1]{0:T(128)}, u32[]{:S(2)}, u32[]{:S(2)}) collective-permute-start(s32[1]{0:T(128)} %param.11), channel_id=1, source_target_pairs={{0,1},{1,2},{2,3},{3,4},{4,5},{5,6},{6,7},{7,8},{8,9},{9,10},{10,1... | collective-permute-start | bytes 20 | tf_op jit(solution)/shard_map/ppermute | solution.py:43
  89.4 2.2 %all-to-all-done.1 = f32[8,64,256]{2,1,0:T(8,128)S(1)} async-done(((f32[8,64,256]{2,1,0:T(8,128)}), f32[8,64,256]{2,1,0:T(8,128)S(1)}, u32[]{:S(2)}, u32[]{:S(2)}) %all-to-all-start.1) | async-done | bytes 524320 | tf_op jit(solution)/shard_map/all_to_all | solution.py:36
  91.8 2.3 %collective-permute-start = (bf16[64,1,64]{2,0,1:T(8,128)(2,1)S(1)}, bf16[64,1,64]{2,0,1:T(8,128)(2,1)S(1)}, u32[]{:S(2)}, u32[]{:S(2)}) collective-permute-start(bf16[64,1,64]{2,0,1:T(8,128)(2,1)S(1)} %copy.180), channel_id=1, source_target_pairs={{0,32},{32,64},{64,96},{96,128},{128,160},{160,192},{192,224},{1,3... | collective-permute-start | bytes 24584 | tf_op jit(solution)/shard_map/ppermute | solution.py:51
  94.1 2.5 %collective-permute-start.1 = (bf16[64,1,64]{2,0,1:T(8,128)(2,1)S(1)}, bf16[64,1,64]{2,0,1:T(8,128)(2,1)S(1)}, u32[]{:S(2)}, u32[]{:S(2)}) collective-permute-start(bf16[64,1,64]{2,0,1:T(8,128)(2,1)S(1)} %copy.181), channel_id=1, source_target_pairs={{32,0},{64,32},{96,64},{128,96},{160,128},{192,160},{224,192},{33,... | collective-permute-start | bytes 24584 | tf_op jit(solution)/shard_map/ppermute | solution.py:54
  96.7 2.5 %collective-permute-done.1 = bf16[64,1,64]{2,0,1:T(8,128)(2,1)S(1)} collective-permute-done((bf16[64,1,64]{2,0,1:T(8,128)(2,1)S(1)}, bf16[64,1,64]{2,0,1:T(8,128)(2,1)S(1)}, u32[]{:S(2)}, u32[]{:S(2)}) %collective-permute-start.1) | collective-permute-done | bytes 8224 | tf_op jit(solution)/shard_map/ppermute | solution.py:54
  99.2 7.1 %collective-permute-start.2 = (bf16[64,6,1]{2,0,1:T(8,128)(2,1)S(1)}, bf16[64,6,1]{2,0,1:T(8,128)(2,1)S(1)}, u32[]{:S(2)}, u32[]{:S(2)}) collective-permute-start(bf16[64,6,1]{2,0,1:T(8,128)(2,1)S(1)} %get-tuple-element.19), channel_id=1, source_target_pairs={{0,1},{1,2},{2,3},{3,4},{4,5},{5,6},{6,7},{7,8},{8,9},{9,10},{10,1... | collective-permute-start | bytes 2312 | tf_op jit(solution)/shard_map/ppermute | solution.py:51
  106.3 1.9 %collective-permute-start.3 = (bf16[64,6,1]{2,0,1:T(8,128)(2,1)S(1)}, bf16[64,6,1]{2,0,1:T(8,128)(2,1)S(1)}, u32[]{:S(2)}, u32[]{:S(2)}) collective-permute-start(bf16[64,6,1]{2,0,1:T(8,128)(2,1)S(1)} %get-tuple-element.20), channel_id=1, source_target_pairs={{1,0},{2,1},{3,2},{4,3},{5,4},{6,5},{7,6},{8,7},{9,8},{10,9},{11,1... | collective-permute-start | bytes 2312 | tf_op jit(solution)/shard_map/ppermute | solution.py:54
  108.4 7.4 %collective-permute-done.3 = bf16[64,6,1]{2,0,1:T(8,128)(2,1)S(1)} collective-permute-done((bf16[64,6,1]{2,0,1:T(8,128)(2,1)S(1)}, bf16[64,6,1]{2,0,1:T(8,128)(2,1)S(1)}, u32[]{:S(2)}, u32[]{:S(2)}) %collective-permute-start.3) | collective-permute-done | bytes 800 | tf_op jit(solution)/shard_map/ppermute | solution.py:54
  116.8 0.4 convolution_add_fusion.15
  117.9 0.4 convolution_add_fusion.12
  118.3 0.4 convolution_add_fusion.11
  119.4 0.4 multiply_bitcast_fusion.1
  121.8 3.7 %collective-permute-start.5 = (bf16[64,1,128]{2,0,1:T(8,128)(2,1)S(1)}, bf16[64,1,128]{2,0,1:T(8,128)(2,1)S(1)}, u32[]{:S(2)}, u32[]{:S(2)}) collective-permute-start(bf16[64,1,128]{2,0,1:T(8,128)(2,1)S(1)} %get-tuple-element.17), channel_id=1, source_target_pairs={{0,32},{32,64},{64,96},{96,128},{128,160},{160,192},{192,224},{1,3... | collective-permute-start | bytes 49160 | tf_op jit(solution)/shard_map/ppermute | solution.py:51
  125.5 1.9 %collective-permute-start.6 = (bf16[64,1,128]{2,0,1:T(8,128)(2,1)S(1)}, bf16[64,1,128]{2,0,1:T(8,128)(2,1)S(1)}, u32[]{:S(2)}, u32[]{:S(2)}) collective-permute-start(bf16[64,1,128]{2,0,1:T(8,128)(2,1)S(1)} %get-tuple-element.18), channel_id=1, source_target_pairs={{32,0},{64,32},{96,64},{128,96},{160,128},{192,160},{224,192},{33,... | collective-permute-start | bytes 49160 | tf_op jit(solution)/shard_map/ppermute | solution.py:54
  127.4 3.1 %collective-permute-done.6 = bf16[64,1,128]{2,0,1:T(8,128)(2,1)S(1)} collective-permute-done((bf16[64,1,128]{2,0,1:T(8,128)(2,1)S(1)}, bf16[64,1,128]{2,0,1:T(8,128)(2,1)S(1)}, u32[]{:S(2)}, u32[]{:S(2)}) %collective-permute-start.6) | collective-permute-done | bytes 16416 | tf_op jit(solution)/shard_map/ppermute | solution.py:54
  130.7 1.9 %collective-permute-start.7 = (bf16[64,10,1]{2,0,1:T(8,128)(2,1)S(1)}, bf16[64,10,1]{2,0,1:T(8,128)(2,1)S(1)}, u32[]{:S(2)}, u32[]{:S(2)}) collective-permute-start(bf16[64,10,1]{2,0,1:T(8,128)(2,1)S(1)} %get-tuple-element.15), channel_id=1, source_target_pairs={{0,1},{1,2},{2,3},{3,4},{4,5},{5,6},{6,7},{7,8},{8,9},{9,10},{10,1... | collective-permute-start | bytes 3848 | tf_op jit(solution)/shard_map/ppermute | solution.py:51
  132.6 3.6 %collective-permute-start.8 = (bf16[64,10,1]{2,0,1:T(8,128)(2,1)S(1)}, bf16[64,10,1]{2,0,1:T(8,128)(2,1)S(1)}, u32[]{:S(2)}, u32[]{:S(2)}) collective-permute-start(bf16[64,10,1]{2,0,1:T(8,128)(2,1)S(1)} %get-tuple-element.16), channel_id=1, source_target_pairs={{1,0},{2,1},{3,2},{4,3},{5,4},{6,5},{7,6},{8,7},{9,8},{10,9},{11,1... | collective-permute-start | bytes 3848 | tf_op jit(solution)/shard_map/ppermute | solution.py:54
  136.2 1.4 collective-permute-done.7
  137.6 5.2 %collective-permute-done.8 = bf16[64,10,1]{2,0,1:T(8,128)(2,1)S(1)} collective-permute-done((bf16[64,10,1]{2,0,1:T(8,128)(2,1)S(1)}, bf16[64,10,1]{2,0,1:T(8,128)(2,1)S(1)}, u32[]{:S(2)}, u32[]{:S(2)}) %collective-permute-start.8) | collective-permute-done | bytes 1312 | tf_op jit(solution)/shard_map/ppermute | solution.py:54
  143.5 0.7 broadcast_in_dim.104
  144.5 0.9 fusion.12
  145.4 0.9 fusion.14
  146.2 0.9 fusion.16
  147.1 0.9 fusion.18
  148.0 0.9 fusion.20
  148.8 0.9 fusion.22
  149.7 0.9 fusion.24
  150.6 0.9 fusion.26
  151.4 1.2 multiply_bitcast_fusion
  153.0 0.4 convolution_add_fusion.7
  153.3 0.4 convolution_add_fusion.6
  154.0 0.4 convolution_add_fusion.4
  154.4 0.4 convolution_add_fusion.3
  155.0 0.4 convolution_add_fusion.1
  155.4 0.4 fusion.8
  155.8 0.5 convolution_bitcast_fusion.2
  156.2 0.6 copy.158
  (80 shorter events, 7.5 us)
Async XLA Ops:
  0.0 155.8 %copy-start = (bf16[3,64]{1,0:T(4,128)(2,1)S(1)}, bf16[3,64]{1,0:T(4,128)(2,1)}, u32[]{:S(2)}) copy-start(bf16[3,64]{1,0:T(4,128)(2,1)} %param.17) | copy-start | bytes 1156
  0.0 3.0 %copy-start.8 = (bf16[2,2,256,256]{3,2,1,0:T(8,128)(2,1)S(1)}, bf16[2,2,256,256]{3,2,1,0:T(8,128)(2,1)}, u32[]{:S(2)}) copy-start(bf16[2,2,256,256]{3,2,1,0:T(8,128)(2,1)} %param.13) | copy-start | bytes 1572868
  0.0 3.0 %copy-start.11 = (bf16[2,32,256]{2,1,0:T(8,128)(2,1)S(1)}, bf16[2,32,256]{2,1,0:T(8,128)(2,1)}, u32[]{:S(2)}) copy-start(bf16[2,32,256]{2,1,0:T(8,128)(2,1)} %param.12) | copy-start | bytes 98308
  7.0 3.5 %copy-start.10 = (bf16[2,256]{1,0:T(2,128)(2,1)S(1)}, bf16[2,256]{1,0:T(2,128)(2,1)}, u32[]{:S(2)}) copy-start(bf16[2,256]{1,0:T(2,128)(2,1)} %param.15) | copy-start | bytes 3076
  10.5 1.9 %copy-start.1 = (bf16[8192,256]{1,0:T(8,128)(2,1)}, bf16[8192,256]{1,0:T(8,128)(2,1)S(1)}, u32[]{:S(2)}) copy-start(bf16[8192,256]{1,0:T(8,128)(2,1)S(1)} %fusion.3) | copy-start | bytes 12582916
  24.6 2.0 %copy-start.2 = (bf16[8192,256]{1,0:T(8,128)(2,1)}, bf16[8192,256]{1,0:T(8,128)(2,1)S(1)}, u32[]{:S(2)}) copy-start(bf16[8192,256]{1,0:T(8,128)(2,1)S(1)} %fusion.5) | copy-start | bytes 12582916
  29.9 9.3 %copy-start.9 = (bf16[2,256,64]{1,2,0:T(8,128)(2,1)S(1)}, bf16[2,256,64]{1,2,0:T(8,128)(2,1)}, u32[]{:S(2)}) copy-start(bf16[2,256,64]{1,2,0:T(8,128)(2,1)} %param.14) | copy-start | bytes 196612
  34.0 42.2 %all-to-all-start = ((f32[8,2,2048]{2,1,0:T(2,128)}), f32[8,2,2048]{2,1,0:T(2,128)S(1)}, u32[]{:S(2)}, u32[]{:S(2)}) async-start(f32[8,2,2048]{2,1,0:T(2,128)} %broadcast_in_dim.91), calls=%async_computation | async-start | bytes 262144 | tf_op jit(solution)/shard_map/all_to_all | solution.py:22
  39.2 3.7 %copy-start.3 = (bf16[8192,256]{1,0:T(8,128)(2,1)S(1)}, bf16[8192,256]{1,0:T(8,128)(2,1)}, u32[]{:S(2)}) copy-start(bf16[8192,256]{1,0:T(8,128)(2,1)} %copy-done.2) | copy-start | bytes 12582916
  48.4 3.9 %copy-start.6 = (f32[2048,4]{1,0:T(8,128)S(1)}, f32[2048,4]{1,0:T(8,128)}, u32[]{:S(2)}) copy-start(f32[2048,4]{1,0:T(8,128)} %get-tuple-element.6) | copy-start | bytes 98308
  52.2 12.5 %copy-start.4 = (f32[64,8192]{0,1:T(8,128)S(1)}, f32[64,8192]{0,1:T(8,128)}, u32[]{:S(2)}) copy-start(f32[64,8192]{0,1:T(8,128)} %copy.132) | copy-start | bytes 6291460
  52.2 12.5 %copy-start.5 = (f32[2048,4]{1,0:T(8,128)S(1)}, f32[2048,4]{1,0:T(8,128)}, u32[]{:S(2)}) copy-start(f32[2048,4]{1,0:T(8,128)} %get-tuple-element.23) | copy-start | bytes 98308
  64.7 11.2 %copy-start.12 = (s32[1,16]{1,0:T(1,128)S(1)}, s32[1,16]{1,0:T(1,128)}, u32[]{:S(2)}) copy-start(s32[1,16]{1,0:T(1,128)} %param.10) | copy-start | bytes 196
  77.3 11.3 %copy-start.7 = (bf16[4,3,3,64,64]{4,3,2,1,0:T(8,128)(2,1)S(1)}, bf16[4,3,3,64,64]{4,3,2,1,0:T(8,128)(2,1)}, u32[]{:S(2)}) copy-start(bf16[4,3,3,64,64]{4,3,2,1,0:T(8,128)(2,1)} %param.16) | copy-start | bytes 884740
  78.5 13.1 %all-to-all-start.1 = ((f32[8,64,256]{2,1,0:T(8,128)}), f32[8,64,256]{2,1,0:T(8,128)S(1)}, u32[]{:S(2)}, u32[]{:S(2)}) async-start(f32[8,64,256]{2,1,0:T(8,128)} %copy.134), calls=%async_computation.1 | async-start | bytes 1048576 | tf_op jit(solution)/shard_map/all_to_all | solution.py:36
  83.3 5.5 %collective-permute-start.4 = (s32[1]{0:T(128)}, s32[1]{0:T(128)}, u32[]{:S(2)}, u32[]{:S(2)}) collective-permute-start(s32[1]{0:T(128)} %param.11), channel_id=1, source_target_pairs={{0,1},{1,2},{2,3},{3,4},{4,5},{5,6},{6,7},{7,8},{8,9},{9,10},{10,1... | collective-permute-start | bytes 20 | tf_op jit(solution)/shard_map/ppermute | solution.py:43
  91.8 4.8 %collective-permute-start = (bf16[64,1,64]{2,0,1:T(8,128)(2,1)S(1)}, bf16[64,1,64]{2,0,1:T(8,128)(2,1)S(1)}, u32[]{:S(2)}, u32[]{:S(2)}) collective-permute-start(bf16[64,1,64]{2,0,1:T(8,128)(2,1)S(1)} %copy.180), channel_id=1, source_target_pairs={{0,32},{32,64},{64,96},{96,128},{128,160},{160,192},{192,224},{1,3... | collective-permute-start | bytes 24584 | tf_op jit(solution)/shard_map/ppermute | solution.py:51
  94.1 5.1 %collective-permute-start.1 = (bf16[64,1,64]{2,0,1:T(8,128)(2,1)S(1)}, bf16[64,1,64]{2,0,1:T(8,128)(2,1)S(1)}, u32[]{:S(2)}, u32[]{:S(2)}) collective-permute-start(bf16[64,1,64]{2,0,1:T(8,128)(2,1)S(1)} %copy.181), channel_id=1, source_target_pairs={{32,0},{64,32},{96,64},{128,96},{160,128},{192,160},{224,192},{33,... | collective-permute-start | bytes 24584 | tf_op jit(solution)/shard_map/ppermute | solution.py:54
  99.2 9.1 %collective-permute-start.2 = (bf16[64,6,1]{2,0,1:T(8,128)(2,1)S(1)}, bf16[64,6,1]{2,0,1:T(8,128)(2,1)S(1)}, u32[]{:S(2)}, u32[]{:S(2)}) collective-permute-start(bf16[64,6,1]{2,0,1:T(8,128)(2,1)S(1)} %get-tuple-element.19), channel_id=1, source_target_pairs={{0,1},{1,2},{2,3},{3,4},{4,5},{5,6},{6,7},{7,8},{8,9},{9,10},{10,1... | collective-permute-start | bytes 2312 | tf_op jit(solution)/shard_map/ppermute | solution.py:51
  106.3 9.4 %collective-permute-start.3 = (bf16[64,6,1]{2,0,1:T(8,128)(2,1)S(1)}, bf16[64,6,1]{2,0,1:T(8,128)(2,1)S(1)}, u32[]{:S(2)}, u32[]{:S(2)}) collective-permute-start(bf16[64,6,1]{2,0,1:T(8,128)(2,1)S(1)} %get-tuple-element.20), channel_id=1, source_target_pairs={{1,0},{2,1},{3,2},{4,3},{5,4},{6,5},{7,6},{8,7},{9,8},{10,9},{11,1... | collective-permute-start | bytes 2312 | tf_op jit(solution)/shard_map/ppermute | solution.py:54
  121.8 5.6 %collective-permute-start.5 = (bf16[64,1,128]{2,0,1:T(8,128)(2,1)S(1)}, bf16[64,1,128]{2,0,1:T(8,128)(2,1)S(1)}, u32[]{:S(2)}, u32[]{:S(2)}) collective-permute-start(bf16[64,1,128]{2,0,1:T(8,128)(2,1)S(1)} %get-tuple-element.17), channel_id=1, source_target_pairs={{0,32},{32,64},{64,96},{96,128},{128,160},{160,192},{192,224},{1,3... | collective-permute-start | bytes 49160 | tf_op jit(solution)/shard_map/ppermute | solution.py:51
  125.5 5.1 %collective-permute-start.6 = (bf16[64,1,128]{2,0,1:T(8,128)(2,1)S(1)}, bf16[64,1,128]{2,0,1:T(8,128)(2,1)S(1)}, u32[]{:S(2)}, u32[]{:S(2)}) collective-permute-start(bf16[64,1,128]{2,0,1:T(8,128)(2,1)S(1)} %get-tuple-element.18), channel_id=1, source_target_pairs={{32,0},{64,32},{96,64},{128,96},{160,128},{192,160},{224,192},{33,... | collective-permute-start | bytes 49160 | tf_op jit(solution)/shard_map/ppermute | solution.py:54
  130.7 6.9 %collective-permute-start.7 = (bf16[64,10,1]{2,0,1:T(8,128)(2,1)S(1)}, bf16[64,10,1]{2,0,1:T(8,128)(2,1)S(1)}, u32[]{:S(2)}, u32[]{:S(2)}) collective-permute-start(bf16[64,10,1]{2,0,1:T(8,128)(2,1)S(1)} %get-tuple-element.15), channel_id=1, source_target_pairs={{0,1},{1,2},{2,3},{3,4},{4,5},{5,6},{6,7},{7,8},{8,9},{9,10},{10,1... | collective-permute-start | bytes 3848 | tf_op jit(solution)/shard_map/ppermute | solution.py:51
  132.6 10.3 %collective-permute-start.8 = (bf16[64,10,1]{2,0,1:T(8,128)(2,1)S(1)}, bf16[64,10,1]{2,0,1:T(8,128)(2,1)S(1)}, u32[]{:S(2)}, u32[]{:S(2)}) collective-permute-start(bf16[64,10,1]{2,0,1:T(8,128)(2,1)S(1)} %get-tuple-element.16), channel_id=1, source_target_pairs={{1,0},{2,1},{3,2},{4,3},{5,4},{6,5},{7,6},{8,7},{9,8},{10,9},{11,1... | collective-permute-start | bytes 3848 | tf_op jit(solution)/shard_map/ppermute | solution.py:54
where the time goes:
time: 158 us; the launch traced here: 157 us
  matrix products  41.8 us (26%)
  starting transfers between devices  39.6 us (25%)
  other arithmetic  30.7 us (19%)
  waiting for transfers between devices  22 us (14%)
  local copies, waits for them, and re-layouts  20.9 us (13%)
  between operations  1.93 us (1%)
    reduce_sum x2, other arithmetic, block_field(): jnp.sum(feature.reshape(feature.shape[0], count, SAMP) * weights[None], a...  23.7 us
    ppermute x4, waiting for transfers between devices, padded_2(): lax.ppermute(lax.slice_in_dim(block, 0, width, axis=dim), axis, backward)  18.2 us
    dot_general x36, matrix products, conv_valid(): lax.dot_general(kernel[down, across], window, (((1,), (0,)), ((), ())), p...  16.4 us
    ppermute x4, starting transfers between devices, padded_2(): lax.ppermute(lax.slice_in_dim(block, block.shape[dim] - width, None, axis...  14.9 us
    ppermute x4, starting transfers between devices, padded_2(): lax.ppermute(lax.slice_in_dim(block, 0, width, axis=dim), axis, backward)  9.95 us
    dot_general x2, matrix products, block_field(): jnp.dot(hidden, w_hidden[0], preferred_element_type=jnp.float32)  8.94 us
    dot_general x2, matrix products, block_field(): jnp.dot(hidden, w_hidden[1], preferred_element_type=jnp.float32)  6.89 us
    dot_general x2, local copies, waits for them, and re-layouts, block_field(): lax.dot_general(w_head, hidden, (((0,), (1,)), ((), ())), preferred_eleme...  6.6 us
  transfers between devices with their start and end apart: 11, of which 8 were waited for; matrix products, arithmetic and copies ran while one was open for 24% of the time, Pallas kernels for 0%

commit v1 on v0

v1 whole, which is shorter than its diff:
```python
import functools

import jax
import jax.numpy as jnp
from jax import lax
from jax.experimental import pallas as pl
from jax.experimental.pallas import tpu as pltpu
from jax.sharding import PartitionSpec as P

f32, bf16 = jnp.float32, jnp.bfloat16
MESH = pl.DeviceIdType.MESH

ENC = 32
SAMP = 4
STEP = 0.03
FEAT = 64
WIDTH = 256
COLS = 64
RAYS = 2048
CHUNK = 1024
PITCH = 128
WINDOW = 512


def iota(shape, dim):
    return lax.broadcasted_iota(jnp.int32, shape, dim)


def relu(x):
    return jnp.maximum(x, 0.0)


def dot(a, b):
    return jnp.dot(a, b, preferred_element_type=f32)


def dot_nt(a, b):
    return lax.dot_general(a, b, (((1,), (1,)), ((), ())), preferred_element_type=f32)


def field_chunk(x, w1, w2, w3, head):
    rays = x.shape[0]
    h = relu(dot_nt(w1, x)).astype(bf16)
    h = jnp.concatenate([h[WIDTH * s : WIDTH * (s + 1)] for s in range(SAMP)], axis=1)
    h = relu(dot(w2, h)).astype(bf16)
    h = relu(dot(w3, h)).astype(bf16)
    out = dot(head, h)
    raw = out[FEAT : FEAT + 1]
    optical = STEP * (jnp.maximum(raw, 0.0) + jnp.log(1.0 + jnp.exp(-jnp.abs(raw))))
    total = jnp.zeros((1, rays), f32)
    colour = jnp.zeros((FEAT, rays), f32)
    for s in range(SAMP):
        here = optical[:, s * rays : (s + 1) * rays]
        weight = jnp.exp(-total) * (1.0 - jnp.exp(-here))
        total = total + here
        colour = colour + weight * out[:FEAT, s * rays : (s + 1) * rays]
    return total, colour


def field_kernel(
    n_block, n_patch, order, seam, x, w_in, w_mid, w_feat, w_dens, window_out, left_out, right_out,
    spread, w1, w2, w3, head, colour, depth, depth_in, part, part_in, own, edges, edge_in,
    depth_send, depth_recv, part_send, part_recv, edge_send, edge_recv,
):
    me = lax.axis_index("block")
    place = lax.axis_index("patch")
    left = lax.rem(place + n_patch - 1, n_patch)
    right = lax.rem(place + 1, n_patch)
    barrier = pltpu.get_barrier_semaphore()
    for k in range(1, n_block):
        pl.semaphore_signal(barrier, inc=1, device_id=(lax.rem(me + k, n_block), place), device_id_type=MESH)
    for side in (left, right):
        pl.semaphore_signal(barrier, inc=1, device_id=(me, side), device_id_type=MESH)

    spread[...] = jnp.zeros_like(spread)
    for m in range(2):
        for s in range(SAMP):
            spread[ENC * s : ENC * (s + 1), WIDTH * s : WIDTH * (s + 1)] = w_in[m]
        w1[m] = spread[...].T
        w2[m] = w_mid[m, 0].T
        w3[m] = w_mid[m, 1].T
        head[m, :FEAT] = w_feat[m].T
        head[m, FEAT:] = jnp.broadcast_to(w_dens[pl.ds(m, 1), :], (16, WIDTH))
    part[:, :128] = jnp.zeros((FEAT, 128), bf16)
    part[:, 128 + RAYS :] = jnp.zeros((FEAT, 128), bf16)

    def chunk(c, carry):
        for m in range(2):
            rows = pl.ds(pl.multiple_of(c * CHUNK, CHUNK), CHUNK)
            total, tint = field_chunk(x[m, rows, :], w1[m], w2[m], w3[m], head[m])
            depth[pl.ds(m, 1), rows] = total
            colour[m, c] = tint
        return carry

    lax.fori_loop(0, RAYS // CHUNK, chunk, 0)

    pl.semaphore_wait(barrier, n_block - 1 + 2)
    depth_copies = []
    for k in range(1, n_block):
        copy = pltpu.make_async_remote_copy(
            src_ref=depth, dst_ref=depth_in.at[k - 1], send_sem=depth_send.at[k - 1],
            recv_sem=depth_recv.at[k - 1], device_id=(lax.rem(me + k, n_block), place), device_id_type=MESH,
        )
        copy.start()
        depth_copies.append(copy)

    def rank_of(first):
        member = first + iota((2, 128), 0)
        rank = jnp.zeros((2, 128), jnp.int32)
        for k in range(16):
            rank = jnp.where(member == order[0, k], k, rank)
        return rank

    mine = rank_of(2 * me)
    thresholds = [mine[m : m + 1] for m in range(2)]
    ranks = [mine] + [rank_of(2 * lax.rem(me + n_block - k, n_block)) for k in range(1, n_block)]
    gates = [[(r < t).astype(f32) for t in thresholds] for r in ranks]
    for copy in depth_copies:
        copy.wait_recv()
    for t in range(RAYS // 128):
        lanes = slice(128 * t, 128 * (t + 1))
        slots = [depth[:, lanes]] + [depth_in[k - 1, :, lanes] for k in range(1, n_block)]
        c, off = t * 128 // CHUNK, t * 128 % CHUNK
        mixed = None
        for m in range(2):
            prefix = sum(slot * gate[m] for slot, gate in zip(slots, gates))
            prefix = prefix[0:1] + prefix[1:2]
            term = jnp.exp(-prefix) * colour[m, c, :, off : off + 128]
            mixed = term if mixed is None else mixed + term
        part[:, 128 + 128 * t : 256 + 128 * t] = mixed.astype(bf16)

    part_copies = []
    for k in range(1, n_block):
        peer = lax.rem(me + k, n_block)
        copy = pltpu.make_async_remote_copy(
            src_ref=part.at[:, pl.ds(pl.multiple_of(256 * peer, 128), WINDOW)], dst_ref=part_in.at[k - 1],
            send_sem=part_send.at[k - 1], recv_sem=part_recv.at[k - 1],
            device_id=(peer, place), device_id_type=MESH,
        )
        copy.start()
        part_copies.append(copy)
    total = part[:, pl.ds(pl.multiple_of(256 * me, 128), WINDOW)].astype(f32)
    link = jnp.where(place < n_patch - 1, seam[0], 0).astype(f32)
    own[FEAT:] = jnp.full((FEAT, WINDOW), link, f32).astype(bf16)
    line = iota((32, WINDOW), 0)
    wanted = (line % 16) // 2 * COLS + line % 2 + jnp.where(line >= 16, COLS - 2, 0)
    pick = (iota((32, WINDOW), 1) == wanted).astype(f32).astype(bf16)
    for k in range(1, n_block):
        part_copies[k - 1].wait_recv()
        total = total + part_in[k - 1].astype(f32)
    window = total.astype(bf16)
    own[:FEAT] = window
    window_out[...] = window
    edges[...] = dot_nt(pick, own[...]).astype(bf16).reshape(2, 16, 128)
    edge_copies = []
    for side, target in ((0, left), (1, right)):
        copy = pltpu.make_async_remote_copy(
            src_ref=edges.at[side], dst_ref=edge_in.at[side], send_sem=edge_send.at[side],
            recv_sem=edge_recv.at[side], device_id=(me, target), device_id_type=MESH,
        )
        copy.start()
        edge_copies.append(copy)
    for copy in edge_copies:
        copy.wait_recv()
    right_out[...] = edge_in[0]
    left_out[...] = edge_in[1]
    for copy in depth_copies + part_copies + edge_copies:
        copy.wait_send()


def field(order, seam, x, w_in, w_mid, w_feat, w_dens, n_block, n_patch):
    vmem = pl.BlockSpec(memory_space=pltpu.VMEM)
    smem = pl.BlockSpec(memory_space=pltpu.SMEM)
    dma = pltpu.SemaphoreType.DMA
    return pl.pallas_call(
        functools.partial(field_kernel, n_block, n_patch),
        out_shape=[
            jax.ShapeDtypeStruct((FEAT, WINDOW), bf16),
            jax.ShapeDtypeStruct((16, 128), bf16),
            jax.ShapeDtypeStruct((16, 128), bf16),
        ],
        in_specs=[smem, smem] + [vmem] * 5,
        out_specs=[vmem] * 3,
        scratch_shapes=[
            pltpu.VMEM((128, 1024), bf16),
            pltpu.VMEM((2, 1024, 128), bf16),
            pltpu.VMEM((2, WIDTH, WIDTH), bf16),
            pltpu.VMEM((2, WIDTH, WIDTH), bf16),
            pltpu.VMEM((2, FEAT + 16, WIDTH), bf16),
            pltpu.VMEM((2, RAYS // CHUNK, FEAT, CHUNK), f32),
            pltpu.VMEM((2, RAYS), f32),
            pltpu.VMEM((n_block - 1, 2, RAYS), f32),
            pltpu.VMEM((FEAT, RAYS + 256), bf16),
            pltpu.VMEM((n_block - 1, FEAT, WINDOW), bf16),
            pltpu.VMEM((2 * FEAT, WINDOW), bf16),
            pltpu.VMEM((2, 16, 128), bf16),
            pltpu.VMEM((2, 16, 128), bf16),
            dma((n_block - 1,)), dma((n_block - 1,)), dma((n_block - 1,)), dma((n_block - 1,)), dma((2,)), dma((2,)),
        ],
        compiler_params=pltpu.CompilerParams(collective_id=0, has_side_effects=True),
        name="field",
    )(order, seam, x, w_in, w_mid, w_feat, w_dens)


def phase_source(phase, tap):
    return (phase + tap - 1) // 2


def put(ref, row, col, value):
    ref[row : row + value.shape[0], col : col + value.shape[1]] = value


def enlarge_weights(ref, w_conv, layer):
    taps = [[w_conv[layer, a, e].astype(f32) for e in range(3)] for a in range(3)]
    for pa in range(2):
        for pb in range(2):
            for dr in range(-1, 2):
                for dc in range(-1, 2):
                    hits = [taps[a][e] for a in range(3) for e in range(3)
                            if phase_source(pa, a) == dr and phase_source(pb, e) == dc]
                    value = sum(hits[1:], hits[0]) if hits else jnp.zeros((FEAT, FEAT), f32)
                    put(ref, (2 * pa + pb) * FEAT, ((dr + 1) * 3 + dc + 1) * FEAT, value.astype(bf16))


def dense_weights(ref, w_conv, layer):
    for qa in range(2):
        for qb in range(2):
            for s in range(-1, 3):
                for t in range(-1, 3):
                    a, e = s - qa + 1, t - qb + 1
                    inside = 0 <= a <= 2 and 0 <= e <= 2
                    value = w_conv[layer, a, e] if inside else jnp.zeros((FEAT, FEAT), bf16)
                    put(ref, (2 * qa + qb) * FEAT, ((s + 1) * 4 + t + 1) * FEAT, value)


def colour_weights(ref, w_conv, w_color, layer):
    ref[...] = jnp.zeros_like(ref)
    for a in range(3):
        for e in range(3):
            tint = dot(w_color[...], w_conv[layer, a, e])
            for i in range(4):
                for j in range(4):
                    group = (i - a + 2) * 6 + (j - e + 2)
                    cell = ((i // 2 * 2 + j // 2) * 2 + i % 2) * 2 + j % 2
                    put(ref, 8 * group, cell * FEAT, tint)


def moved(x, by):
    return pltpu.roll(x, (-by) % x.shape[1], 1)


def lines(x, first, count):
    return x[:, first * PITCH : (first + count) * PITCH]


def decoder_kernel(n_block, n_patch, seam, window, left_edge, right_edge, w_conv, w_color, out, k0, k1, k2, k3, res):
    me = lax.axis_index("block")
    place = lax.axis_index("patch")
    enlarge_weights(k0, w_conv, 0)
    dense_weights(k1, w_conv, 1)
    enlarge_weights(k2, w_conv, 2)
    colour_weights(k3, w_conv, w_color, 3)

    lane = iota((1, PITCH), 1)
    right_open = jnp.where(place < n_patch - 1, seam[0], 0).astype(f32)
    left_open = left_edge[0:1, FEAT : FEAT + 1].astype(f32)
    inner = jnp.where(lane < 2, left_open, jnp.where(lane < COLS + 2, 1.0, jnp.where(lane < COLS + 4, right_open, 0.0)))
    top = inner * jnp.where(me > 0, 1.0, 0.0)
    bottom = inner * jnp.where(me < n_block - 1, 1.0, 0.0)
    mask = jnp.concatenate([top] + [inner] * 4 + [bottom], axis=1)

    source = iota((128, 256), 0)
    move = (iota((128, 256), 1) == source // COLS * PITCH + source % COLS + 2).astype(f32).astype(bf16)
    body = jnp.concatenate([window[:, 128 * t : 128 * (t + 1)] for t in range(4)], axis=0)
    body = dot(body, move)
    image = jnp.concatenate([body[FEAT * t : FEAT * (t + 1)] for t in range(4)], axis=1)
    source = iota((32, 8 * PITCH), 0)
    target = (source % 16) // 2 * PITCH + source % 2 + jnp.where(source >= 16, COLS + 2, 0)
    halo_move = (iota((32, 8 * PITCH), 1) == target).astype(f32).astype(bf16)
    halo = jnp.concatenate([left_edge[...], right_edge[...]], axis=0).astype(f32).T
    image = image + dot(halo[:FEAT].astype(bf16), halo_move)
    image = image * jnp.concatenate([inner] * 8, axis=1)

    views = {-1: moved(image, -1).astype(bf16), 0: image.astype(bf16), 1: moved(image, 1).astype(bf16)}
    patches = jnp.concatenate([lines(views[dc], 1 + dr, 6) for dr in range(-1, 2) for dc in range(-1, 2)], axis=0)
    first = relu(dot(k0[...], patches)) * mask

    def column_views(maps):
        cell = lambda a, b: maps[(2 * a + b) * FEAT : (2 * a + b + 1) * FEAT]
        return [{-1: moved(cell(a, 1), -1).astype(bf16), 0: cell(a, 0).astype(bf16), 1: cell(a, 1).astype(bf16),
                 2: moved(cell(a, 0), 1).astype(bf16)} for a in range(2)]

    views = column_views(first)
    empty = jnp.zeros((FEAT, PITCH), bf16)
    parts = []
    for s in range(-1, 3):
        for t in range(-1, 3):
            view = views[s % 2][t]
            if s == -1:
                view = jnp.concatenate([empty, lines(view, 0, 5)], axis=1)
            if s == 2:
                view = jnp.concatenate([lines(view, 1, 5), empty], axis=1)
            parts.append(view)
    second = relu(dot(k1[...], jnp.concatenate(parts, axis=0))) * mask

    views = column_views(second)
    parts = []
    for qa in range(2):
        for qb in range(2):
            cells = []
            for s in range(qa - 1, qa + 2):
                for t in range(qb - 1, qb + 2):
                    start = s // 2 + 1 - qa
                    cells.append(lines(views[s % 2][t], start, 5))
            third = relu(dot(k2[...], jnp.concatenate(cells, axis=0))) * lines(mask, 1 - qa, 5)
            third = third.astype(bf16)
            blank = jnp.zeros((4 * FEAT, PITCH), bf16)
            parts.append(jnp.concatenate([third, blank] if qa else [blank, third], axis=1))
    spread = dot(k3[...].astype(bf16), jnp.concatenate(parts, axis=0))

    def cell(i, j):
        group = (i + 1) * 6 + j + 1
        return spread[8 * group : 8 * group + 8]

    def row(i, j):
        value = lines(cell(i, j), 1, 4)
        if i == 0:
            value = value + lines(cell(4, j), 0, 4)
        if i == 3:
            value = value + lines(cell(-1, j), 2, 4)
        return value

    stack = []
    for i in range(4):
        cols = [row(i, j) for j in range(-1, 5)]
        middle = cols[1:5]
        middle[0] = middle[0] + moved(cols[5], -1)
        middle[3] = middle[3] + moved(cols[0], 1)
        stack.append(middle)
    wide = jnp.concatenate(
        [jnp.concatenate([lines(stack[i][j], r, 1) for j in range(4)], axis=1) for r in range(4) for i in range(4)], axis=0
    )
    source = iota((4 * PITCH, 256), 0)
    at = source % PITCH - 2
    target = jnp.where((at >= 0) & (at < COLS), 4 * at + source // PITCH, -1)
    weave = (iota((4 * PITCH, 256), 1) == target).astype(f32).astype(bf16)
    high = wide.astype(bf16)
    low = (wide - high.astype(f32)).astype(bf16)
    woven = dot(high, weave) + dot(low, weave)
    for half in range(2):
        lanes = slice(128 * half, 128 * (half + 1))
        res[half] = woven[:, lanes]
        for k in range(3):
            out[k, :, lanes] = res[half, pl.ds(k, 16, stride=8), :]


def decoder(seam, window, left_edge, right_edge, w_conv, w_color, n_block, n_patch):
    vmem = pl.BlockSpec(memory_space=pltpu.VMEM)
    return pl.pallas_call(
        functools.partial(decoder_kernel, n_block, n_patch),
        out_shape=jax.ShapeDtypeStruct((3, 16, 256), f32),
        in_specs=[pl.BlockSpec(memory_space=pltpu.SMEM)] + [vmem] * 5,
        out_specs=vmem,
        scratch_shapes=[
            pltpu.VMEM((256, 576), bf16),
            pltpu.VMEM((256, 1024), bf16),
            pltpu.VMEM((256, 576), bf16),
            pltpu.VMEM((288, 1024), f32),
            pltpu.VMEM((2, 128, 128), f32),
        ],
        name="decoder",
    )(seam, window, left_edge, right_edge, w_conv, w_color)


def body(samples_in, block_order, seam_link, w_in, w_mid, w_feat, w_density, w_conv, w_color):
    n_block, n_patch = lax.axis_size("block"), lax.axis_size("patch")
    x = samples_in.reshape(2, RAYS, SAMP * ENC)
    window, left_edge, right_edge = field(block_order, seam_link, x, w_in, w_mid, w_feat, w_density, n_block, n_patch)
    return decoder(seam_link, window, left_edge, right_edge, w_conv, w_color, n_block, n_patch)


def solution(mesh):
    return jax.shard_map(
        body,
        mesh=mesh,
        in_specs=(
            P("block", None, "patch", None),
            P("patch", None),
            P("patch"),
            P("block", None, None),
            P("block", None, None, None),
            P("block", None, None),
            P("block", None),
            P(),
            P(),
        ),
        out_specs=P(None, "block", "patch"),
        check_vma=False,
    )
```

time: 158 us -> 42.4 us (0.27)
  the two profiles are of different devices: /device:TPU:111 before, /device:TPU:1 now
where the time goes in v1:
time: 42.4 us; the launch traced here: 42.2 us
  Pallas kernels  40 us (94%)
  local copies, waits for them, and re-layouts  1.6 us (4%)
  between operations  0.66 us (2%)
    pallas_call x1, Pallas kernels, field(): pl.pallas_call(functools.partial(field_kernel, n_block, n_patch), out_sha...  34.3 us
    pallas_call x1, Pallas kernels, decoder(): pl.pallas_call(functools.partial(decoder_kernel, n_block, n_patch), out_s...  5.62 us
    unnamed x1, local copies, waits for them, and re-layouts  1.6 us

profile of v1, /device:TPU:1, one launch (start us, length us, event | category | flops | bytes accessed | tf_op | source)
XLA Modules:
  0.0 42.2 jit_solution(18143164464963804626)
XLA Ops:
  0.7 1.6 %copy.10.w_feat = bf16[2,256,64]{2,1,0:T(8,128)(2,1)} copy(bf16[2,256,64]{1,2,0:T(8,128)(2,1)} %param.14) | data formatting | bytes 131072 | tf_op args[5]
  2.2 34.3 %field.1 = (bf16[64,512]{1,0:T(8,128)(2,1)}, bf16[16,128]{1,0:T(8,128)(2,1)}, bf16[16,128]{1,0:T(8,128)(2,1)}) custom-call(s32[1,16]{1,0:T(1,128)} %order.1, s32[1]{0:T(128)S(6)} %copy.11.seam, bf16[2,2048,128]{2,1,0:T(8,128)(2,1)} %bitcast.1, bf16[2,32,256]{2,1,0:T(8,128)(2,1)} %w_in.1, bf16[2,2,256,256]{3,2,1,0:T(8,128)(2,1)} %w_mid.1, ...), custom_call_target="tpu_custom_call" | custom-call | tf_op jit(solution)/shard_map/field/pallas_call | solution.py:175
  36.6 5.6 %decoder.1 = f32[3,16,256]{2,1,0:T(8,128)} custom-call(s32[1]{0:T(128)S(6)} %copy.11.seam, bf16[64,512]{1,0:T(8,128)(2,1)} %get-tuple-element.8.window, bf16[16,128]{1,0:T(8,128)(2,1)} %get-tuple-element.9.left_edge, bf16[16,128]{1,0:T(8,128)(2,1)} %get-tuple-element.10.right_edge, bf16[4,3,3,64,64]{4,3,2,1,0:T(8,128)(2,1)} %w_conv.1, bf16[3,64]{1,0:T(4,128)(2,1)} %w_color.1), custom_call_target="tpu_custom_call" | custom-call | tf_op jit(solution)/shard_map/decoder/pallas_call | solution.py:359

commit v2 on v1

--- a/solution.py
+++ b/solution.py
@@ -66,11 +66,17 @@
     place = lax.axis_index("patch")
     left = lax.rem(place + n_patch - 1, n_patch)
     right = lax.rem(place + 1, n_patch)
+    edge_in[...] = jnp.zeros_like(edge_in)
     barrier = pltpu.get_barrier_semaphore()
     for k in range(1, n_block):
         pl.semaphore_signal(barrier, inc=1, device_id=(lax.rem(me + k, n_block), place), device_id_type=MESH)
-    for side in (left, right):
-        pl.semaphore_signal(barrier, inc=1, device_id=(me, side), device_id_type=MESH)
+    sides = ((left, place > 0), (right, place < n_patch - 1))
+    for side, there in sides:
+
+        @pl.when(there)
+        def _():
+            pl.semaphore_signal(barrier, inc=1, device_id=(me, side), device_id_type=MESH)
+
 
     spread[...] = jnp.zeros_like(spread)
     for m in range(2):
@@ -79,7 +85,7 @@
         w1[m] = spread[...].T
         w2[m] = w_mid[m, 0].T
         w3[m] = w_mid[m, 1].T
-        head[m, :FEAT] = w_feat[m].T
+        head[m, :FEAT] = w_feat[m]
         head[m, FEAT:] = jnp.broadcast_to(w_dens[pl.ds(m, 1), :], (16, WIDTH))
     part[:, :128] = jnp.zeros((FEAT, 128), bf16)
     part[:, 128 + RAYS :] = jnp.zeros((FEAT, 128), bf16)
@@ -94,7 +100,8 @@
 
     lax.fori_loop(0, RAYS // CHUNK, chunk, 0)
 
-    pl.semaphore_wait(barrier, n_block - 1 + 2)
+    count = (place > 0).astype(jnp.int32) + (place < n_patch - 1).astype(jnp.int32)
+    pl.semaphore_wait(barrier, n_block - 1 + count)
     depth_copies = []
     for k in range(1, n_block):
         copy = pltpu.make_async_remote_copy(
@@ -152,20 +159,23 @@
     own[:FEAT] = window
     window_out[...] = window
     edges[...] = dot_nt(pick, own[...]).astype(bf16).reshape(2, 16, 128)
-    edge_copies = []
-    for side, target in ((0, left), (1, right)):
-        copy = pltpu.make_async_remote_copy(
+    edge_copies = [
+        pltpu.make_async_remote_copy(
             src_ref=edges.at[side], dst_ref=edge_in.at[side], send_sem=edge_send.at[side],
-            recv_sem=edge_recv.at[side], device_id=(me, target), device_id_type=MESH,
+            recv_sem=edge_recv.at[side], device_id=(me, sides[side][0]), device_id_type=MESH,
         )
-        copy.start()
-        edge_copies.append(copy)
-    for copy in edge_copies:
-        copy.wait_recv()
+        for side in range(2)
+    ]
+    for side in range(2):
+        pl.when(sides[side][1])(edge_copies[side].start)
+    for side in range(2):
+        pl.when(sides[1 - side][1])(edge_copies[side].wait_recv)
     right_out[...] = edge_in[0]
     left_out[...] = edge_in[1]
-    for copy in depth_copies + part_copies + edge_copies:
+    for copy in depth_copies + part_copies:
         copy.wait_send()
+    for side in range(2):
+        pl.when(sides[side][1])(edge_copies[side].wait_send)
 
 
 def field(order, seam, x, w_in, w_mid, w_feat, w_dens, n_block, n_patch):
@@ -375,7 +385,9 @@
 def body(samples_in, block_order, seam_link, w_in, w_mid, w_feat, w_density, w_conv, w_color):
     n_block, n_patch = lax.axis_size("block"), lax.axis_size("patch")
     x = samples_in.reshape(2, RAYS, SAMP * ENC)
-    window, left_edge, right_edge = field(block_order, seam_link, x, w_in, w_mid, w_feat, w_density, n_block, n_patch)
+    window, left_edge, right_edge = field(
+        block_order, seam_link, x, w_in, w_mid, jnp.swapaxes(w_feat, 1, 2), w_density, n_block, n_patch
+    )
     return decoder(seam_link, window, left_edge, right_edge, w_conv, w_color, n_block, n_patch)
 
 

time: 42.4 us -> 35.3 us (0.83)
  the two profiles are of different devices: /device:TPU:1 before, /device:TPU:225 now
where the time goes in v2:
time: 35.3 us; the launch traced here: 35.1 us
  Pallas kernels  34.4 us (97%)
  between operations  0.66 us (2%)
    pallas_call x1, Pallas kernels, field(): pl.pallas_call(functools.partial(field_kernel, n_block, n_patch), out_sha...  28.8 us
    pallas_call x1, Pallas kernels, decoder(): pl.pallas_call(functools.partial(decoder_kernel, n_block, n_patch), out_s...  5.63 us

profile of v2, /device:TPU:225, one launch (start us, length us, event | category | flops | bytes accessed | tf_op | source)
XLA Modules:
  0.0 35.1 jit_solution(1192406219715769705)
XLA Ops:
  0.7 28.8 %field.1 = (bf16[64,512]{1,0:T(8,128)(2,1)}, bf16[16,128]{1,0:T(8,128)(2,1)}, bf16[16,128]{1,0:T(8,128)(2,1)}) custom-call(s32[1,16]{1,0:T(1,128)} %order.1, s32[1]{0:T(128)S(6)} %copy.10.seam, bf16[2,2048,128]{2,1,0:T(8,128)(2,1)} %bitcast.2, bf16[2,32,256]{2,1,0:T(8,128)(2,1)} %w_in.1, bf16[2,2,256,256]{3,2,1,0:T(8,128)(2,1)} %w_mid.1, ...), custom_call_target="tpu_custom_call" | custom-call | tf_op jit(solution)/shard_map/field/pallas_call | solution.py:185
  29.4 5.6 %decoder.1 = f32[3,16,256]{2,1,0:T(8,128)} custom-call(s32[1]{0:T(128)S(6)} %copy.10.seam, bf16[64,512]{1,0:T(8,128)(2,1)} %get-tuple-element.8.window, bf16[16,128]{1,0:T(8,128)(2,1)} %get-tuple-element.9.left_edge, bf16[16,128]{1,0:T(8,128)(2,1)} %get-tuple-element.10.right_edge, bf16[4,3,3,64,64]{4,3,2,1,0:T(8,128)(2,1)} %w_conv.1, bf16[3,64]{1,0:T(4,128)(2,1)} %w_color.1), custom_call_target="tpu_custom_call" | custom-call | tf_op jit(solution)/shard_map/decoder/pallas_call | solution.py:369

commit v3 on v2

--- a/solution.py
+++ b/solution.py
@@ -17,9 +17,7 @@
 WIDTH = 256
 COLS = 64
 RAYS = 2048
-CHUNK = 1024
 PITCH = 128
-WINDOW = 512
 
 
 def iota(shape, dim):
@@ -57,26 +55,47 @@
     return total, colour
 
 
+def tile_of(device, unit):
+    parity, late = unit // 2, unit % 2
+    apart = (device + parity) % 2
+    tile = device + (1 - 2 * late) * apart
+    return (tile - parity + 8) // 2 % 4
+
+
 def field_kernel(
-    n_block, n_patch, order, seam, x, w_in, w_mid, w_feat, w_dens, window_out, left_out, right_out,
-    spread, w1, w2, w3, head, colour, depth, depth_in, part, part_in, own, edges, edge_in,
-    depth_send, depth_recv, part_send, part_recv, edge_send, edge_recv,
+    n_block, n_patch, order, seam, x, w_in, w_mid, w_feat, w_dens, window_out, halo_out, link_out,
+    spread, w1, w2, w3, head, rays_out, rays_in, meta, meta_in, colour, depth, colour_in, depth_in, lines16,
+    rays_send, rays_recv, meta_send, meta_recv, colour_send, colour_recv, depth_send, depth_recv,
 ):
     me = lax.axis_index("block")
     place = lax.axis_index("patch")
-    left = lax.rem(place + n_patch - 1, n_patch)
-    right = lax.rem(place + 1, n_patch)
-    edge_in[...] = jnp.zeros_like(edge_in)
+    sides = ((place - 1, place > 0), (place + 1, place < n_patch - 1))
+    rays_in[...] = jnp.zeros_like(rays_in)
+    meta_in[...] = jnp.zeros_like(meta_in)
     barrier = pltpu.get_barrier_semaphore()
     for k in range(1, n_block):
-        pl.semaphore_signal(barrier, inc=1, device_id=(lax.rem(me + k, n_block), place), device_id_type=MESH)
-    sides = ((left, place > 0), (right, place < n_patch - 1))
+        pl.semaphore_signal(barrier, inc=1, device_id=((me + k) % n_block, place), device_id_type=MESH)
     for side, there in sides:
 
         @pl.when(there)
         def _():
             pl.semaphore_signal(barrier, inc=1, device_id=(me, side), device_id_type=MESH)
 
+    line = iota((16, 256), 0)
+    wanted = line % 8 // 2 * COLS + line % 2 + jnp.where(line >= 8, COLS - 2, 0)
+    pick = (iota((16, 256), 1) == wanted).astype(f32).astype(bf16)
+    for m in range(2):
+        found = [dot(pick, x[m, 2 * g : 2 * g + 2].reshape(256, 128)) for g in range(8)]
+        for side in range(2):
+            rows = jnp.concatenate([f[8 * side : 8 * side + 8] for f in found], axis=0)
+            rays_out[side, m] = rows.astype(bf16)
+    slot = iota((16, 128), 0)
+    member = 2 * ((me + n_block - slot // 2) % n_block) + slot % 2
+    rank = jnp.zeros((16, 128), jnp.int32)
+    for k in range(16):
+        rank = jnp.where(member == order[0, k], k, rank)
+    meta[:16] = rank
+    meta[16:] = jnp.full((8, 128), jnp.where(place < n_patch - 1, seam[0], 0), jnp.int32)
 
     spread[...] = jnp.zeros_like(spread)
     for m in range(2):
@@ -87,95 +106,105 @@
         w3[m] = w_mid[m, 1].T
         head[m, :FEAT] = w_feat[m]
         head[m, FEAT:] = jnp.broadcast_to(w_dens[pl.ds(m, 1), :], (16, WIDTH))
-    part[:, :128] = jnp.zeros((FEAT, 128), bf16)
-    part[:, 128 + RAYS :] = jnp.zeros((FEAT, 128), bf16)
-
-    def chunk(c, carry):
+
+    def side_copies(side):
+        target = (me, sides[side][0])
+        return [
+            pltpu.make_async_remote_copy(
+                src_ref=rays_out.at[side], dst_ref=rays_in.at[1 - side], send_sem=rays_send.at[side],
+                recv_sem=rays_recv.at[1 - side], device_id=target, device_id_type=MESH,
+            ),
+            pltpu.make_async_remote_copy(
+                src_ref=meta, dst_ref=meta_in.at[1 - side], send_sem=meta_send.at[side],
+                recv_sem=meta_recv.at[1 - side], device_id=target, device_id_type=MESH,
+            ),
+        ]
+
+    def send(unit, m, tiles):
+        for k in range(1, n_block):
+            peer = (me + k) % n_block
+            tile = tile_of(peer, unit) if tiles > 1 else 0
+            for src, dst, ssem, rsem in (
+                (colour, colour_in, colour_send, colour_recv), (depth, depth_in, depth_send, depth_recv),
+            ):
+                pltpu.make_async_remote_copy(
+                    src_ref=src.at[unit, m, tile], dst_ref=dst.at[unit, m, k - 1], send_sem=ssem.at[unit, m],
+                    recv_sem=rsem.at[unit, m], device_id=(peer, place), device_id_type=MESH,
+                ).start()
+
+    def compute(unit, m, rays, tiles):
+        total, tint = field_chunk(rays, w1[m], w2[m], w3[m], head[m])
+        tint = tint.astype(bf16)
+        for j in range(tiles):
+            depth[unit, m, j] = total[:, 128 * j : 128 * (j + 1)]
+            colour[unit, m, j] = tint[:, 128 * j : 128 * (j + 1)]
+
+    def full(unit, first):
         for m in range(2):
-            rows = pl.ds(pl.multiple_of(c * CHUNK, CHUNK), CHUNK)
-            total, tint = field_chunk(x[m, rows, :], w1[m], w2[m], w3[m], head[m])
-            depth[pl.ds(m, 1), rows] = total
-            colour[m, c] = tint
+            compute(unit, m, jnp.concatenate([x[m, 4 * j + unit] for j in range(4)], axis=0), 4)
+            if first is not None and m == 0:
+
+                @pl.when(first)
+                def _():
+                    count = (place > 0).astype(jnp.int32) + (place < n_patch - 1).astype(jnp.int32)
+                    pl.semaphore_wait(barrier, n_block - 1 + count)
+                    for side in range(2):
+                        for copy in side_copies(side):
+                            pl.when(sides[side][1])(copy.start)
+
+            send(unit, m, 4)
+
+    def loop(unit, carry):
+        full(unit, unit == 0)
         return carry
 
-    lax.fori_loop(0, RAYS // CHUNK, chunk, 0)
-
-    count = (place > 0).astype(jnp.int32) + (place < n_patch - 1).astype(jnp.int32)
-    pl.semaphore_wait(barrier, n_block - 1 + count)
-    depth_copies = []
-    for k in range(1, n_block):
-        copy = pltpu.make_async_remote_copy(
-            src_ref=depth, dst_ref=depth_in.at[k - 1], send_sem=depth_send.at[k - 1],
-            recv_sem=depth_recv.at[k - 1], device_id=(lax.rem(me + k, n_block), place), device_id_type=MESH,
-        )
-        copy.start()
-        depth_copies.append(copy)
-
-    def rank_of(first):
-        member = first + iota((2, 128), 0)
-        rank = jnp.zeros((2, 128), jnp.int32)
-        for k in range(16):
-            rank = jnp.where(member == order[0, k], k, rank)
-        return rank
-
-    mine = rank_of(2 * me)
-    thresholds = [mine[m : m + 1] for m in range(2)]
-    ranks = [mine] + [rank_of(2 * lax.rem(me + n_block - k, n_block)) for k in range(1, n_block)]
-    gates = [[(r < t).astype(f32) for t in thresholds] for r in ranks]
-    for copy in depth_copies:
-        copy.wait_recv()
-    for t in range(RAYS // 128):
-        lanes = slice(128 * t, 128 * (t + 1))
-        slots = [depth[:, lanes]] + [depth_in[k - 1, :, lanes] for k in range(1, n_block)]
-        c, off = t * 128 // CHUNK, t * 128 % CHUNK
-        mixed = None
+    lax.fori_loop(0, 3, loop, 0)
+    for side in range(2):
+        for copy in side_copies(side):
+            pl.when(sides[1 - side][1])(copy.wait_recv)
+    for m in range(2):
+        compute(4, m, jnp.concatenate([rays_in[0, m], rays_in[1, m]], axis=0), 1)
+        send(4, m, 1)
+    full(3, None)
+
+    def combine(unit, tile, ranks):
         for m in range(2):
-            prefix = sum(slot * gate[m] for slot, gate in zip(slots, gates))
-            prefix = prefix[0:1] + prefix[1:2]
-            term = jnp.exp(-prefix) * colour[m, c, :, off : off + 128]
-            mixed = term if mixed is None else mixed + term
-        part[:, 128 + 128 * t : 256 + 128 * t] = mixed.astype(bf16)
-
-    part_copies = []
-    for k in range(1, n_block):
-        peer = lax.rem(me + k, n_block)
-        copy = pltpu.make_async_remote_copy(
-            src_ref=part.at[:, pl.ds(pl.multiple_of(256 * peer, 128), WINDOW)], dst_ref=part_in.at[k - 1],
-            send_sem=part_send.at[k - 1], recv_sem=part_recv.at[k - 1],
-            device_id=(peer, place), device_id_type=MESH,
-        )
-        copy.start()
-        part_copies.append(copy)
-    total = part[:, pl.ds(pl.multiple_of(256 * me, 128), WINDOW)].astype(f32)
-    link = jnp.where(place < n_patch - 1, seam[0], 0).astype(f32)
-    own[FEAT:] = jnp.full((FEAT, WINDOW), link, f32).astype(bf16)
-    line = iota((32, WINDOW), 0)
-    wanted = (line % 16) // 2 * COLS + line % 2 + jnp.where(line >= 16, COLS - 2, 0)
-    pick = (iota((32, WINDOW), 1) == wanted).astype(f32).astype(bf16)
-    for k in range(1, n_block):
-        part_copies[k - 1].wait_recv()
-        total = total + part_in[k - 1].astype(f32)
-    window = total.astype(bf16)
-    own[:FEAT] = window
-    window_out[...] = window
-    edges[...] = dot_nt(pick, own[...]).astype(bf16).reshape(2, 16, 128)
-    edge_copies = [
-        pltpu.make_async_remote_copy(
-            src_ref=edges.at[side], dst_ref=edge_in.at[side], send_sem=edge_send.at[side],
-            recv_sem=edge_recv.at[side], device_id=(me, sides[side][0]), device_id_type=MESH,
-        )
-        for side in range(2)
-    ]
+            for got, sem in ((colour_in, colour_recv), (depth_in, depth_recv)):
+                pltpu.make_async_copy(got.at[unit, m], got.at[unit, m], sem.at[unit, m]).wait()
+            lines16[m : m + 1] = depth[unit, m, tile]
+            for k in range(1, n_block):
+                lines16[2 * k + m : 2 * k + m + 1] = depth_in[unit, m, k - 1]
+        depths = lines16[...]
+        mixed = jnp.zeros((FEAT, 128), f32)
+        for i in range(16):
+            k, m = i // 2, i % 2
+            prefix = jnp.sum(jnp.where(ranks < ranks[i : i + 1], depths, 0.0), axis=0, keepdims=True)
+            tint = colour[unit, m, tile] if k == 0 else colour_in[unit, m, k - 1]
+            mixed = mixed + jnp.exp(-prefix) * tint.astype(f32)
+        return mixed
+
+    def own_tile(unit):
+        mixed = combine(unit, tile_of(me, unit), meta[:16])
+        late = unit % 2
+        apart = (me + unit // 2) % 2
+        at = 1 + late + (2 - 4 * late) * apart
+        outside = ((at == 0) & (me == 0)) | ((at == 3) & (me == n_block - 1))
+        window_out[at] = (mixed * jnp.where(outside, 0.0, 1.0)).astype(bf16)
+
+    for unit in range(3):
+        own_tile(unit)
+    ranks = jnp.where(iota((16, 128), 1) < 64, meta_in[0, :16], meta_in[1, :16])
+    halo_out[...] = combine(4, 0, ranks).astype(bf16)
+    link_out[...] = meta_in[0, 16:]
+    own_tile(3)
+
     for side in range(2):
-        pl.when(sides[side][1])(edge_copies[side].start)
-    for side in range(2):
-        pl.when(sides[1 - side][1])(edge_copies[side].wait_recv)
-    right_out[...] = edge_in[0]
-    left_out[...] = edge_in[1]
-    for copy in depth_copies + part_copies:
-        copy.wait_send()
-    for side in range(2):
-        pl.when(sides[side][1])(edge_copies[side].wait_send)
+        for copy in side_copies(side):
+            pl.when(sides[side][1])(copy.wait_send)
+    for unit in range(5):
+        for m in range(2):
+            for got, sem in ((colour_in, colour_send), (depth_in, depth_send)):
+                pltpu.make_async_copy(got.at[unit, m], got.at[unit, m], sem.at[unit, m]).wait()
 
 
 def field(order, seam, x, w_in, w_mid, w_feat, w_dens, n_block, n_patch):
@@ -185,9 +214,9 @@
     return pl.pallas_call(
         functools.partial(field_kernel, n_block, n_patch),
         out_shape=[
-            jax.ShapeDtypeStruct((FEAT, WINDOW), bf16),
-            jax.ShapeDtypeStruct((16, 128), bf16),
-            jax.ShapeDtypeStruct((16, 128), bf16),
+            jax.ShapeDtypeStruct((4, FEAT, 128), bf16),
+            jax.ShapeDtypeStruct((FEAT, 128), bf16),
+            jax.ShapeDtypeStruct((8, 128), jnp.int32),
         ],
         in_specs=[smem, smem] + [vmem] * 5,
         out_specs=[vmem] * 3,
@@ -197,15 +226,16 @@
             pltpu.VMEM((2, WIDTH, WIDTH), bf16),
             pltpu.VMEM((2, WIDTH, WIDTH), bf16),
             pltpu.VMEM((2, FEAT + 16, WIDTH), bf16),
-            pltpu.VMEM((2, RAYS // CHUNK, FEAT, CHUNK), f32),
-            pltpu.VMEM((2, RAYS), f32),
-            pltpu.VMEM((n_block - 1, 2, RAYS), f32),
-            pltpu.VMEM((FEAT, RAYS + 256), bf16),
-            pltpu.VMEM((n_block - 1, FEAT, WINDOW), bf16),
-            pltpu.VMEM((2 * FEAT, WINDOW), bf16),
-            pltpu.VMEM((2, 16, 128), bf16),
-            pltpu.VMEM((2, 16, 128), bf16),
-            dma((n_block - 1,)), dma((n_block - 1,)), dma((n_block - 1,)), dma((n_block - 1,)), dma((2,)), dma((2,)),
+            pltpu.VMEM((2, 2, 64, 128), bf16),
+            pltpu.VMEM((2, 2, 64, 128), bf16),
+            pltpu.VMEM((24, 128), jnp.int32),
+            pltpu.VMEM((2, 24, 128), jnp.int32),
+            pltpu.VMEM((5, 2, 4, FEAT, 128), bf16),
+            pltpu.VMEM((5, 2, 4, 1, 128), f32),
+            pltpu.VMEM((5, 2, n_block - 1, FEAT, 128), bf16),
+            pltpu.VMEM((5, 2, n_block - 1, 1, 128), f32),
+            pltpu.VMEM((16, 128), f32),
+            dma((2,)), dma((2,)), dma((2,)), dma((2,)), dma((5, 2)), dma((5, 2)), dma((5, 2)), dma((5, 2)),
         ],
         compiler_params=pltpu.CompilerParams(collective_id=0, has_side_effects=True),
         name="field",
@@ -263,7 +293,7 @@
     return x[:, first * PITCH : (first + count) * PITCH]
 
 
-def decoder_kernel(n_block, n_patch, seam, window, left_edge, right_edge, w_conv, w_color, out, k0, k1, k2, k3, res):
+def decoder_kernel(n_block, n_patch, seam, window, halo, link, w_conv, w_color, out, k0, k1, k2, k3, res):
     me = lax.axis_index("block")
     place = lax.axis_index("patch")
     enlarge_weights(k0, w_conv, 0)
@@ -273,7 +303,7 @@
 
     lane = iota((1, PITCH), 1)
     right_open = jnp.where(place < n_patch - 1, seam[0], 0).astype(f32)
-    left_open = left_edge[0:1, FEAT : FEAT + 1].astype(f32)
+    left_open = link[0:1].astype(f32)
     inner = jnp.where(lane < 2, left_open, jnp.where(lane < COLS + 2, 1.0, jnp.where(lane < COLS + 4, right_open, 0.0)))
     top = inner * jnp.where(me > 0, 1.0, 0.0)
     bottom = inner * jnp.where(me < n_block - 1, 1.0, 0.0)
@@ -281,14 +311,14 @@
 
     source = iota((128, 256), 0)
     move = (iota((128, 256), 1) == source // COLS * PITCH + source % COLS + 2).astype(f32).astype(bf16)
-    body = jnp.concatenate([window[:, 128 * t : 128 * (t + 1)] for t in range(4)], axis=0)
-    body = dot(body, move)
+    body = dot(window[...].reshape(4 * FEAT, 128), move)
     image = jnp.concatenate([body[FEAT * t : FEAT * (t + 1)] for t in range(4)], axis=1)
-    source = iota((32, 8 * PITCH), 0)
-    target = (source % 16) // 2 * PITCH + source % 2 + jnp.where(source >= 16, COLS + 2, 0)
-    halo_move = (iota((32, 8 * PITCH), 1) == target).astype(f32).astype(bf16)
-    halo = jnp.concatenate([left_edge[...], right_edge[...]], axis=0).astype(f32).T
-    image = image + dot(halo[:FEAT].astype(bf16), halo_move)
+    source = iota((128, 8 * PITCH), 0)
+    row = source % 64 // 2 - 4 * me + 2
+    target = row * PITCH + source % 2 + jnp.where(source >= 64, COLS + 2, 0)
+    target = jnp.where((row >= 0) & (row < 8), target, -1)
+    halo_move = (iota((128, 8 * PITCH), 1) == target).astype(f32).astype(bf16)
+    image = image + dot(halo[...], halo_move)
     image = image * jnp.concatenate([inner] * 8, axis=1)
 
     views = {-1: moved(image, -1).astype(bf16), 0: image.astype(bf16), 1: moved(image, 1).astype(bf16)}
@@ -364,7 +394,7 @@
             out[k, :, lanes] = res[half, pl.ds(k, 16, stride=8), :]
 
 
-def decoder(seam, window, left_edge, right_edge, w_conv, w_color, n_block, n_patch):
+def decoder(seam, window, halo, link, w_conv, w_color, n_block, n_patch):
     vmem = pl.BlockSpec(memory_space=pltpu.VMEM)
     return pl.pallas_call(
         functools.partial(decoder_kernel, n_block, n_patch),
@@ -379,16 +409,16 @@
             pltpu.VMEM((2, 128, 128), f32),
         ],
         name="decoder",
-    )(seam, window, left_edge, right_edge, w_conv, w_color)
+    )(seam, window, halo, link, w_conv, w_color)
 
 
 def body(samples_in, block_order, seam_link, w_in, w_mid, w_feat, w_density, w_conv, w_color):
     n_block, n_patch = lax.axis_size("block"), lax.axis_size("patch")
-    x = samples_in.reshape(2, RAYS, SAMP * ENC)
-    window, left_edge, right_edge = field(
+    x = samples_in.reshape(2, RAYS // 128, 128, SAMP * ENC)
+    window, halo, link = field(
         block_order, seam_link, x, w_in, w_mid, jnp.swapaxes(w_feat, 1, 2), w_density, n_block, n_patch
     )
-    return decoder(seam_link, window, left_edge, right_edge, w_conv, w_color, n_block, n_patch)
+    return decoder(seam_link, window, halo, link, w_conv, w_color, n_block, n_patch)
 
 
 def solution(mesh):

time: 35.3 us -> 31 us (0.88)
  Pallas kernels: 34.4 us -> 30.2 us
    pallas_call x1, Pallas kernels: 28.8 us -> 24.7 us  [field(): pl.pallas_call(functools.partial(field_kernel, n_block, n_patch), out_sha...]
where the time goes in v3:
time: 31 us; the launch traced here: 30.9 us
  Pallas kernels  30.2 us (97%)
  between operations  0.66 us (2%)
    pallas_call x1, Pallas kernels, field(): pl.pallas_call(functools.partial(field_kernel, n_block, n_patch), out_sha...  24.7 us
    pallas_call x1, Pallas kernels, decoder(): pl.pallas_call(functools.partial(decoder_kernel, n_block, n_patch), out_s...  5.54 us

profile of v3, /device:TPU:225, one launch (start us, length us, event | category | flops | bytes accessed | tf_op | source)
XLA Modules:
  0.0 30.9 jit_solution(11131276973918835969)
XLA Ops:
  0.7 24.7 %field.1 = (bf16[4,64,128]{2,1,0:T(8,128)(2,1)}, bf16[64,128]{1,0:T(8,128)(2,1)}, s32[8,128]{1,0:T(8,128)}) custom-call(s32[1,16]{1,0:T(1,128)} %order.1, s32[1]{0:T(128)S(6)} %copy.10.seam, bf16[2,16,128,128]{3,2,1,0:T(8,128)(2,1)} %bitcast.2, bf16[2,32,256]{2,1,0:T(8,128)(2,1)} %w_in.1, bf16[2,2,256,256]{3,2,1,0:T(8,128)(2,1)} %w_mid.1, ...), custom_call_target="tpu_custom_call" | custom-call | tf_op jit(solution)/shard_map/field/pallas_call | solution.py:214
  25.3 5.5 %decoder.1 = f32[3,16,256]{2,1,0:T(8,128)} custom-call(s32[1]{0:T(128)S(6)} %copy.10.seam, bf16[4,64,128]{2,1,0:T(8,128)(2,1)} %get-tuple-element.8.window, bf16[64,128]{1,0:T(8,128)(2,1)} %get-tuple-element.9.halo, s32[8,128]{1,0:T(8,128)} %get-tuple-element.10.link, bf16[4,3,3,64,64]{4,3,2,1,0:T(8,128)(2,1)} %w_conv.1, bf16[3,64]{1,0:T(4,128)(2,1)} %w_color.1), custom_call_target="tpu_custom_call" | custom-call | tf_op jit(solution)/shard_map/decoder/pallas_call | solution.py:399

commit v4 on v3

--- a/solution.py
+++ b/solution.py
@@ -36,36 +36,39 @@
     return lax.dot_general(a, b, (((1,), (1,)), ((), ())), preferred_element_type=f32)
 
 
-def field_chunk(x, w1, w2, w3, head):
-    rays = x.shape[0]
-    h = relu(dot_nt(w1, x)).astype(bf16)
-    h = jnp.concatenate([h[WIDTH * s : WIDTH * (s + 1)] for s in range(SAMP)], axis=1)
-    h = relu(dot(w2, h)).astype(bf16)
-    h = relu(dot(w3, h)).astype(bf16)
-    out = dot(head, h)
-    raw = out[FEAT : FEAT + 1]
-    optical = STEP * (jnp.maximum(raw, 0.0) + jnp.log(1.0 + jnp.exp(-jnp.abs(raw))))
-    total = jnp.zeros((1, rays), f32)
-    colour = jnp.zeros((FEAT, rays), f32)
-    for s in range(SAMP):
-        here = optical[:, s * rays : (s + 1) * rays]
-        weight = jnp.exp(-total) * (1.0 - jnp.exp(-here))
-        total = total + here
-        colour = colour + weight * out[:FEAT, s * rays : (s + 1) * rays]
-    return total, colour
-
-
-def tile_of(device, unit):
-    parity, late = unit // 2, unit % 2
-    apart = (device + parity) % 2
-    tile = device + (1 - 2 * late) * apart
-    return (tile - parity + 8) // 2 % 4
+def field_chunks(streams):
+    count = len(streams)
+    hs = [relu(dot_nt(w1, x)).astype(bf16) for x, w1, w2, w3, head in streams]
+    hs = [jnp.concatenate([h[WIDTH * s : WIDTH * (s + 1)] for s in range(SAMP)], axis=1) for h in hs]
+    hs = [relu(dot(streams[i][2], hs[i])).astype(bf16) for i in range(count)]
+    hs = [relu(dot(streams[i][3], hs[i])).astype(bf16) for i in range(count)]
+    outs = [dot(streams[i][4], hs[i]) for i in range(count)]
+    results = []
+    for out in outs:
+        rays = out.shape[1] // SAMP
+        raw = out[FEAT : FEAT + 1]
+        optical = STEP * (jnp.maximum(raw, 0.0) + jnp.log(1.0 + jnp.exp(-jnp.abs(raw))))
+        total = jnp.zeros((1, rays), f32)
+        colour = jnp.zeros((FEAT, rays), f32)
+        for s in range(SAMP):
+            here = optical[:, s * rays : (s + 1) * rays]
+            weight = jnp.exp(-total) * (1.0 - jnp.exp(-here))
+            total = total + here
+            colour = colour + weight * out[:FEAT, s * rays : (s + 1) * rays]
+        results.append((total, colour))
+    return results
+
+
+def last_tile(device):
+    return ((device + 1) // 2 + 3) % 4
 
 
 def field_kernel(
     n_block, n_patch, order, seam, x, w_in, w_mid, w_feat, w_dens, window_out, halo_out, link_out,
-    spread, w1, w2, w3, head, rays_out, rays_in, meta, meta_in, colour, depth, colour_in, depth_in, lines16,
-    rays_send, rays_recv, meta_send, meta_recv, colour_send, colour_recv, depth_send, depth_recv,
+    spread, w1, w2, w3, head, rays_out, rays_in, meta, meta_in, depth_rows, tiles, tiles_in, last_in, passed, passed_in,
+    halo, halo_in, halo_depth, halo_depth_in, lines16, shares,
+    rays_send, rays_recv, meta_send, meta_recv, tile_send, tile_recv, last_send, last_recv, pass_send, pass_recv,
+    halo_send, halo_recv,
 ):
     me = lax.axis_index("block")
     place = lax.axis_index("patch")
@@ -106,6 +109,7 @@
         w3[m] = w_mid[m, 1].T
         head[m, :FEAT] = w_feat[m]
         head[m, FEAT:] = jnp.broadcast_to(w_dens[pl.ds(m, 1), :], (16, WIDTH))
+    depth_rows[...] = jnp.zeros_like(depth_rows)
 
     def side_copies(side):
         target = (me, sides[side][0])
@@ -120,102 +124,220 @@
             ),
         ]
 
-    def send(unit, m, tiles):
-        for k in range(1, n_block):
-            peer = (me + k) % n_block
-            tile = tile_of(peer, unit) if tiles > 1 else 0
-            for src, dst, ssem, rsem in (
-                (colour, colour_in, colour_send, colour_recv), (depth, depth_in, depth_send, depth_recv),
-            ):
+    def weights(m):
+        return w1[m], w2[m], w3[m], head[m]
+
+    def depth_block(m, total):
+        lanes = slice(0, total.shape[1])
+        high = total.astype(bf16).astype(f32)
+        depth_rows[m : m + 1, lanes] = high
+        depth_rows[2 + m : 3 + m, lanes] = total - high
+
+    def rays_of(unit, m):
+        return jnp.concatenate([x[m, 4 * j + unit] for j in range(4)], axis=0)
+
+    def keep(unit, m, tint):
+        tint = tint.astype(bf16)
+        for j in range(4):
+            tiles[unit, j, FEAT * m : FEAT * (m + 1)] = tint[:, 128 * j : 128 * (j + 1)]
+
+    def keep_depth(unit):
+        rows = depth_rows[...].astype(bf16)
+        for j in range(4):
+            tiles[unit, j, 2 * FEAT :] = rows[:, 128 * j : 128 * (j + 1)]
+
+    def loop(unit, carry):
+        results = field_chunks([(rays_of(unit, m), *weights(m)) for m in range(2)])
+        for m, (total, tint) in enumerate(results):
+            keep(unit, m, tint)
+            depth_block(m, total)
+        keep_depth(unit)
+
+        @pl.when(unit == 0)
+        def _():
+            count = (place > 0).astype(jnp.int32) + (place < n_patch - 1).astype(jnp.int32)
+            pl.semaphore_wait(barrier, n_block - 1 + count)
+            for side in range(2):
+                for copy in side_copies(side):
+                    pl.when(sides[side][1])(copy.start)
+
+        for j in range(4):
+            owner = 2 * j + unit // 2
+
+            @pl.when(owner != me)
+            def _():
                 pltpu.make_async_remote_copy(
-                    src_ref=src.at[unit, m, tile], dst_ref=dst.at[unit, m, k - 1], send_sem=ssem.at[unit, m],
-                    recv_sem=rsem.at[unit, m], device_id=(peer, place), device_id_type=MESH,
+                    src_ref=tiles.at[unit, j], dst_ref=tiles_in.at[unit, (owner + n_block - me) % n_block - 1],
+                    send_sem=tile_send.at[unit], recv_sem=tile_recv.at[unit],
+                    device_id=(owner, place), device_id_type=MESH,
                 ).start()
 
-    def compute(unit, m, rays, tiles):
-        total, tint = field_chunk(rays, w1[m], w2[m], w3[m], head[m])
-        tint = tint.astype(bf16)
-        for j in range(tiles):
-            depth[unit, m, j] = total[:, 128 * j : 128 * (j + 1)]
-            colour[unit, m, j] = tint[:, 128 * j : 128 * (j + 1)]
-
-    def full(unit, first):
-        for m in range(2):
-            compute(unit, m, jnp.concatenate([x[m, 4 * j + unit] for j in range(4)], axis=0), 4)
-            if first is not None and m == 0:
-
-                @pl.when(first)
-                def _():
-                    count = (place > 0).astype(jnp.int32) + (place < n_patch - 1).astype(jnp.int32)
-                    pl.semaphore_wait(barrier, n_block - 1 + count)
-                    for side in range(2):
-                        for copy in side_copies(side):
-                            pl.when(sides[side][1])(copy.start)
-
-            send(unit, m, 4)
-
-    def loop(unit, carry):
-        full(unit, unit == 0)
         return carry
 
     lax.fori_loop(0, 3, loop, 0)
+
     for side in range(2):
         for copy in side_copies(side):
             pl.when(sides[1 - side][1])(copy.wait_recv)
+    results = field_chunks([(jnp.concatenate([rays_in[0, m], rays_in[1, m]], axis=0), *weights(m)) for m in range(2)])
+    for m, (total, tint) in enumerate(results):
+        depth_block(m, total)
+    halo_depth[...] = depth_rows[:, :128].astype(bf16)
+    ray = iota((144, 128), 0) - 8
+    source = jnp.where((ray >= 0) & (ray < 128), ray // 2 % 2 * 64 + ray // 4 * 2 + ray % 2, -1)
+    turn = (iota((144, 128), 1) == source).astype(f32).astype(bf16)
+    both = jnp.concatenate([tint for total, tint in results], axis=0).astype(bf16)
+    halo[...] = dot_nt(turn, both).astype(bf16)
+
+    def halo_copies(k):
+        peer = (me + k) % n_block
+        return [
+            pltpu.make_async_remote_copy(
+                src_ref=halo.at[pl.ds(pl.multiple_of(16 * peer, 16), 32)], dst_ref=halo_in.at[k - 1],
+                send_sem=halo_send.at[0, k - 1], recv_sem=halo_recv.at[0, k - 1],
+                device_id=(peer, place), device_id_type=MESH,
+            ),
+            pltpu.make_async_remote_copy(
+                src_ref=halo_depth, dst_ref=halo_depth_in.at[k - 1],
+                send_sem=halo_send.at[1, k - 1], recv_sem=halo_recv.at[1, k - 1],
+                device_id=(peer, place), device_id_type=MESH,
+            ),
+        ]
+
+    for k in range(1, n_block):
+        for copy in halo_copies(k):
+            copy.start()
+
+    def last_copy(k, m):
+        peer = (me + k) % n_block
+        rows = pl.ds(0, FEAT) if m == 0 else pl.ds(FEAT, FEAT + 8)
+        return pltpu.make_async_remote_copy(
+            src_ref=tiles.at[3, last_tile(peer), rows], dst_ref=last_in.at[k - 1, rows],
+            send_sem=last_send.at[m, k - 1], recv_sem=last_recv.at[m, k - 1],
+            device_id=(peer, place), device_id_type=MESH,
+        )
+
     for m in range(2):
-        compute(4, m, jnp.concatenate([rays_in[0, m], rays_in[1, m]], axis=0), 1)
-        send(4, m, 1)
-    full(3, None)
-
-    def combine(unit, tile, ranks):
-        for m in range(2):
-            for got, sem in ((colour_in, colour_recv), (depth_in, depth_recv)):
-                pltpu.make_async_copy(got.at[unit, m], got.at[unit, m], sem.at[unit, m]).wait()
-            lines16[m : m + 1] = depth[unit, m, tile]
-            for k in range(1, n_block):
-                lines16[2 * k + m : 2 * k + m + 1] = depth_in[unit, m, k - 1]
+        ((total, tint),) = field_chunks([(rays_of(3, m), *weights(m))])
+        keep(3, m, tint)
+        depth_block(m, total)
+        if m == 1:
+            keep_depth(3)
+        for k in range(1, n_block):
+            last_copy(k, m).start()
+
+    def order_weights(blocks, ranks):
+        for k, block in enumerate(blocks):
+            block = block.astype(f32)
+            lines16[2 * k : 2 * k + 2] = block[0:2] + block[2:4]
         depths = lines16[...]
+        prefixes = [
+            jnp.sum(jnp.where(ranks < ranks[i : i + 1], depths, 0.0), axis=0, keepdims=True) for i in range(16)
+        ]
+        return [jnp.exp(-prefix) for prefix in prefixes]
+
+    def combine(own, got):
+        slots = [own] + [got.at[k - 1] for k in range(1, n_block)]
+        factors = order_weights([slot[2 * FEAT :] for slot in slots], meta[:16])
         mixed = jnp.zeros((FEAT, 128), f32)
         for i in range(16):
-            k, m = i // 2, i % 2
-            prefix = jnp.sum(jnp.where(ranks < ranks[i : i + 1], depths, 0.0), axis=0, keepdims=True)
-            tint = colour[unit, m, tile] if k == 0 else colour_in[unit, m, k - 1]
-            mixed = mixed + jnp.exp(-prefix) * tint.astype(f32)
+            tint = slots[i // 2][i % 2 * FEAT : (i % 2 + 1) * FEAT]
+            mixed = mixed + factors[i] * tint.astype(f32)
         return mixed
 
-    def own_tile(unit):
-        mixed = combine(unit, tile_of(me, unit), meta[:16])
-        late = unit % 2
-        apart = (me + unit // 2) % 2
-        at = 1 + late + (2 - 4 * late) * apart
-        outside = ((at == 0) & (me == 0)) | ((at == 3) & (me == n_block - 1))
-        window_out[at] = (mixed * jnp.where(outside, 0.0, 1.0)).astype(bf16)
+    def pass_copy(unit):
+        target = me - 1 if unit % 2 == 0 else me + 1
+        return pltpu.make_async_remote_copy(
+            src_ref=passed.at[unit], dst_ref=passed_in.at[unit], send_sem=pass_send.at[unit],
+            recv_sem=pass_recv.at[unit], device_id=(target, place), device_id_type=MESH,
+        )
+
+    def mine(unit):
+        return me % 2 == unit // 2
+
+    def has_target(unit):
+        return mine(unit) & ((me > 0) if unit % 2 == 0 else (me < n_block - 1))
+
+    def has_source(unit):
+        return (me % 2 != unit // 2) & ((me < n_block - 1) if unit % 2 == 0 else (me > 0))
 
     for unit in range(3):
-        own_tile(unit)
+
+        @pl.when(mine(unit))
+        def _():
+            pltpu.make_async_copy(tiles_in.at[unit], tiles_in.at[unit], tile_recv.at[unit]).wait()
+            passed[unit] = combine(tiles.at[unit, me // 2], tiles_in.at[unit]).astype(bf16)
+
+        pl.when(has_target(unit))(pass_copy(unit).start)
+
+        @pl.when(mine(unit))
+        def _():
+            window_out[1 + unit % 2] = passed[unit]
+
+    for k in range(1, n_block):
+        for copy in halo_copies(k):
+            copy.wait_recv()
     ranks = jnp.where(iota((16, 128), 1) < 64, meta_in[0, :16], meta_in[1, :16])
-    halo_out[...] = combine(4, 0, ranks).astype(bf16)
+    factors = order_weights([halo_depth[...]] + [halo_depth_in[k - 1] for k in range(1, n_block)], ranks)
+    for i in range(16):
+        shares[i : i + 1] = factors[i]
+    line = iota((32, 128), 0)
+    row = line // 4 + 4 * me - 2
+    source = jnp.where((row >= 0) & (row < 32), line // 2 % 2 * 64 + row * 2 + line % 2, -1)
+    turn = (iota((32, 128), 1) == source).astype(f32).astype(bf16)
+    high = shares[...].astype(bf16)
+    low = (shares[...] - high.astype(f32)).astype(bf16)
+    share = dot_nt(turn, high) + dot_nt(turn, low)
+    mixed = jnp.zeros((32, 128), f32)
+    for k in range(n_block):
+        tint = halo[pl.ds(pl.multiple_of(16 * me, 16), 32), :] if k == 0 else halo_in[k - 1]
+        factor = jnp.where(iota((32, 128), 1) < 64, share[:, 2 * k : 2 * k + 1], share[:, 2 * k + 1 : 2 * k + 2])
+        mixed = mixed + factor * tint.astype(f32)
+    halo_out[...] = (mixed + pltpu.roll(mixed, 64, 1)).astype(bf16)
     link_out[...] = meta_in[0, 16:]
-    own_tile(3)
+
+    for unit in range(3):
+
+        @pl.when(has_source(unit))
+        def _():
+            pass_copy(unit).wait_recv()
+            window_out[3 - unit % 2 * 3] = passed_in[unit]
+
+    @pl.when(me == n_block - 1)
+    def _():
+        window_out[3] = jnp.zeros((FEAT, 128), bf16)
+
+    for m in range(2):
+        for k in range(1, n_block):
+            last_copy(k, m).wait_recv()
+    mixed = combine(tiles.at[3, last_tile(me)], last_in)
+    window_out[me % 2 * 2] = (mixed * jnp.where(me > 0, 1.0, 0.0)).astype(bf16)
 
     for side in range(2):
         for copy in side_copies(side):
             pl.when(sides[side][1])(copy.wait_send)
-    for unit in range(5):
-        for m in range(2):
-            for got, sem in ((colour_in, colour_send), (depth_in, depth_send)):
-                pltpu.make_async_copy(got.at[unit, m], got.at[unit, m], sem.at[unit, m]).wait()
+    for k in range(1, n_block):
+        for copy in halo_copies(k) + [last_copy(k, 0), last_copy(k, 1)]:
+            copy.wait_send()
+    for unit in range(3):
+        pl.when(has_target(unit))(pass_copy(unit).wait_send)
+        sent = pltpu.make_async_copy(tiles_in.at[unit, pl.ds(0, 3)], tiles_in.at[unit, pl.ds(0, 3)], tile_send.at[unit])
+        more = pltpu.make_async_copy(tiles_in.at[unit, 3], tiles_in.at[unit, 3], tile_send.at[unit])
+        sent.wait()
+        pl.when(me % 2 != unit // 2)(more.wait)
 
 
 def field(order, seam, x, w_in, w_mid, w_feat, w_dens, n_block, n_patch):
     vmem = pl.BlockSpec(memory_space=pltpu.VMEM)
     smem = pl.BlockSpec(memory_space=pltpu.SMEM)
     dma = pltpu.SemaphoreType.DMA
+    peers = n_block - 1
+    rows = 2 * FEAT + 8
     return pl.pallas_call(
         functools.partial(field_kernel, n_block, n_patch),
         out_shape=[
             jax.ShapeDtypeStruct((4, FEAT, 128), bf16),
-            jax.ShapeDtypeStruct((FEAT, 128), bf16),
+            jax.ShapeDtypeStruct((32, 128), bf16),
             jax.ShapeDtypeStruct((8, 128), jnp.int32),
         ],
         in_specs=[smem, smem] + [vmem] * 5,
@@ -230,12 +352,20 @@
             pltpu.VMEM((2, 2, 64, 128), bf16),
             pltpu.VMEM((24, 128), jnp.int32),
             pltpu.VMEM((2, 24, 128), jnp.int32),
-            pltpu.VMEM((5, 2, 4, FEAT, 128), bf16),
-            pltpu.VMEM((5, 2, 4, 1, 128), f32),
-            pltpu.VMEM((5, 2, n_block - 1, FEAT, 128), bf16),
-            pltpu.VMEM((5, 2, n_block - 1, 1, 128), f32),
+            pltpu.VMEM((8, 512), f32),
+            pltpu.VMEM((4, 4, rows, 128), bf16),
+            pltpu.VMEM((3, peers, rows, 128), bf16),
+            pltpu.VMEM((peers, rows, 128), bf16),
+            pltpu.VMEM((3, FEAT, 128), bf16),
+            pltpu.VMEM((3, FEAT, 128), bf16),
+            pltpu.VMEM((144, 128), bf16),
+            pltpu.VMEM((peers, 32, 128), bf16),
+            pltpu.VMEM((8, 128), bf16),
+            pltpu.VMEM((peers, 8, 128), bf16),
             pltpu.VMEM((16, 128), f32),
-            dma((2,)), dma((2,)), dma((2,)), dma((2,)), dma((5, 2)), dma((5, 2)), dma((5, 2)), dma((5, 2)),
+            pltpu.VMEM((16, 128), f32),
+            dma((2,)), dma((2,)), dma((2,)), dma((2,)), dma((3,)), dma((3,)), dma((2, peers)), dma((2, peers)),
+            dma((3,)), dma((3,)), dma((2, peers)), dma((2, peers)),
         ],
         compiler_params=pltpu.CompilerParams(collective_id=0, has_side_effects=True),
         name="field",
@@ -313,12 +443,10 @@
     move = (iota((128, 256), 1) == source // COLS * PITCH + source % COLS + 2).astype(f32).astype(bf16)
     body = dot(window[...].reshape(4 * FEAT, 128), move)
     image = jnp.concatenate([body[FEAT * t : FEAT * (t + 1)] for t in range(4)], axis=1)
-    source = iota((128, 8 * PITCH), 0)
-    row = source % 64 // 2 - 4 * me + 2
-    target = row * PITCH + source % 2 + jnp.where(source >= 64, COLS + 2, 0)
-    target = jnp.where((row >= 0) & (row < 8), target, -1)
-    halo_move = (iota((128, 8 * PITCH), 1) == target).astype(f32).astype(bf16)
-    image = image + dot(halo[...], halo_move)
+    source = iota((32, 8 * PITCH), 0)
+    target = source // 4 * PITCH + source % 2 + source // 2 % 2 * (COLS + 2)
+    halo_move = (iota((32, 8 * PITCH), 1) == target).astype(f32).astype(bf16)
+    image = image + dot(halo[...].astype(f32).T[:FEAT].astype(bf16), halo_move)
     image = image * jnp.concatenate([inner] * 8, axis=1)
 
     views = {-1: moved(image, -1).astype(bf16), 0: image.astype(bf16), 1: moved(image, 1).astype(bf16)}

time: 31 us -> 27 us (0.87)
  Pallas kernels: 30.2 us -> 26 us
    pallas_call x1, Pallas kernels: 24.7 us -> 20.4 us  [field(): pl.pallas_call(functools.partial(field_kernel, n_block, n_patch), out_sha...]
where the time goes in v4:
time: 27 us; the launch traced here: 26.7 us
  Pallas kernels  26 us (96%)
  between operations  0.66 us (2%)
    pallas_call x1, Pallas kernels, field(): pl.pallas_call(functools.partial(field_kernel, n_block, n_patch), out_sha...  20.4 us
    pallas_call x1, Pallas kernels, decoder(): pl.pallas_call(functools.partial(decoder_kernel, n_block, n_patch), out_s...  5.64 us

profile of v4, /device:TPU:225, one launch (start us, length us, event | category | flops | bytes accessed | tf_op | source)
XLA Modules:
  0.0 26.7 jit_solution(1431565776361986687)
XLA Ops:
  0.7 20.4 %field.1 = (bf16[4,64,128]{2,1,0:T(8,128)(2,1)}, bf16[32,128]{1,0:T(8,128)(2,1)}, s32[8,128]{1,0:T(8,128)}) custom-call(s32[1,16]{1,0:T(1,128)} %order.1, s32[1]{0:T(128)S(6)} %copy.10.seam, bf16[2,16,128,128]{3,2,1,0:T(8,128)(2,1)} %bitcast.2, bf16[2,32,256]{2,1,0:T(8,128)(2,1)} %w_in.1, bf16[2,2,256,256]{3,2,1,0:T(8,128)(2,1)} %w_mid.1, ...), custom_call_target="tpu_custom_call" | custom-call | tf_op jit(solution)/shard_map/field/pallas_call | solution.py:336
  21.1 5.6 %decoder.1 = f32[3,16,256]{2,1,0:T(8,128)} custom-call(s32[1]{0:T(128)S(6)} %copy.10.seam, bf16[4,64,128]{2,1,0:T(8,128)(2,1)} %get-tuple-element.8.window, bf16[32,128]{1,0:T(8,128)(2,1)} %get-tuple-element.9.halo, s32[8,128]{1,0:T(8,128)} %get-tuple-element.10.link, bf16[4,3,3,64,64]{4,3,2,1,0:T(8,128)(2,1)} %w_conv.1, bf16[3,64]{1,0:T(4,128)(2,1)} %w_color.1), custom_call_target="tpu_custom_call" | custom-call | tf_op jit(solution)/shard_map/decoder/pallas_call | solution.py:527

commit v5 on v4

--- a/solution.py
+++ b/solution.py
@@ -59,12 +59,166 @@
     return results
 
 
+def phase_source(phase, tap):
+    return (phase + tap - 1) // 2
+
+
+def put(ref, row, col, value):
+    ref[row : row + value.shape[0], col : col + value.shape[1]] = value
+
+
+def enlarge_weights(ref, w_conv, layer):
+    taps = [[w_conv[layer, a, e].astype(f32) for e in range(3)] for a in range(3)]
+    for pa in range(2):
+        for pb in range(2):
+            for dr in range(-1, 2):
+                for dc in range(-1, 2):
+                    hits = [taps[a][e] for a in range(3) for e in range(3)
+                            if phase_source(pa, a) == dr and phase_source(pb, e) == dc]
+                    value = sum(hits[1:], hits[0]) if hits else jnp.zeros((FEAT, FEAT), f32)
+                    put(ref, (2 * pa + pb) * FEAT, ((dr + 1) * 3 + dc + 1) * FEAT, value.astype(bf16))
+
+
+def dense_weights(ref, w_conv, layer):
+    for qa in range(2):
+        for qb in range(2):
+            for s in range(-1, 3):
+                for t in range(-1, 3):
+                    a, e = s - qa + 1, t - qb + 1
+                    inside = 0 <= a <= 2 and 0 <= e <= 2
+                    value = w_conv[layer, a, e] if inside else jnp.zeros((FEAT, FEAT), bf16)
+                    put(ref, (2 * qa + qb) * FEAT, ((s + 1) * 4 + t + 1) * FEAT, value)
+
+
+def colour_weights(ref, w_conv, w_color, layer):
+    ref[...] = jnp.zeros_like(ref)
+    for a in range(3):
+        for e in range(3):
+            tint = dot(w_color[...], w_conv[layer, a, e])
+            for i in range(4):
+                for j in range(4):
+                    group = (i - a + 2) * 6 + (j - e + 2)
+                    cell = ((i // 2 * 2 + j // 2) * 2 + i % 2) * 2 + j % 2
+                    put(ref, 8 * group, cell * FEAT, tint)
+
+
+def moved(x, by):
+    return pltpu.roll(x, (-by) % x.shape[1], 1)
+
+
+def lines(x, first, count):
+    return x[:, first * PITCH : (first + count) * PITCH]
+
+
+def prepare(w_conv, w_color, k0, k1, k2, k3):
+    enlarge_weights(k0, w_conv, 0)
+    dense_weights(k1, w_conv, 1)
+    enlarge_weights(k2, w_conv, 2)
+    colour_weights(k3, w_conv, w_color, 3)
+
+
+def decode(n_block, n_patch, seam, window, halo, link, out, k0, k1, k2, k3, res):
+    me = lax.axis_index("block")
+    place = lax.axis_index("patch")
+
+    lane = iota((1, PITCH), 1)
+    right_open = jnp.where(place < n_patch - 1, seam[0], 0).astype(f32)
+    left_open = link[0:1].astype(f32)
+    inner = jnp.where(lane < 2, left_open, jnp.where(lane < COLS + 2, 1.0, jnp.where(lane < COLS + 4, right_open, 0.0)))
+    top = inner * jnp.where(me > 0, 1.0, 0.0)
+    bottom = inner * jnp.where(me < n_block - 1, 1.0, 0.0)
+    mask = jnp.concatenate([top] + [inner] * 4 + [bottom], axis=1)
+
+    source = iota((128, 256), 0)
+    move = (iota((128, 256), 1) == source // COLS * PITCH + source % COLS + 2).astype(f32).astype(bf16)
+    body = dot(window[...].reshape(4 * FEAT, 128), move)
+    image = jnp.concatenate([body[FEAT * t : FEAT * (t + 1)] for t in range(4)], axis=1)
+    source = iota((32, 8 * PITCH), 0)
+    target = source // 4 * PITCH + source % 2 + source // 2 % 2 * (COLS + 2)
+    halo_move = (iota((32, 8 * PITCH), 1) == target).astype(f32).astype(bf16)
+    image = image + dot(halo[...].astype(f32).T[:FEAT].astype(bf16), halo_move)
+    image = image * jnp.concatenate([inner] * 8, axis=1)
+
+    views = {-1: moved(image, -1).astype(bf16), 0: image.astype(bf16), 1: moved(image, 1).astype(bf16)}
+    patches = jnp.concatenate([lines(views[dc], 1 + dr, 6) for dr in range(-1, 2) for dc in range(-1, 2)], axis=0)
+    first = relu(dot(k0[...], patches)) * mask
+
+    def column_views(maps):
+        cell = lambda a, b: maps[(2 * a + b) * FEAT : (2 * a + b + 1) * FEAT]
+        return [{-1: moved(cell(a, 1), -1).astype(bf16), 0: cell(a, 0).astype(bf16), 1: cell(a, 1).astype(bf16),
+                 2: moved(cell(a, 0), 1).astype(bf16)} for a in range(2)]
+
+    views = column_views(first)
+    empty = jnp.zeros((FEAT, PITCH), bf16)
+    parts = []
+    for s in range(-1, 3):
+        for t in range(-1, 3):
+            view = views[s % 2][t]
+            if s == -1:
+                view = jnp.concatenate([empty, lines(view, 0, 5)], axis=1)
+            if s == 2:
+                view = jnp.concatenate([lines(view, 1, 5), empty], axis=1)
+            parts.append(view)
+    second = relu(dot(k1[...], jnp.concatenate(parts, axis=0))) * mask
+
+    views = column_views(second)
+    parts = []
+    for qa in range(2):
+        for qb in range(2):
+            cells = []
+            for s in range(qa - 1, qa + 2):
+                for t in range(qb - 1, qb + 2):
+                    start = s // 2 + 1 - qa
+                    cells.append(lines(views[s % 2][t], start, 5))
+            third = relu(dot(k2[...], jnp.concatenate(cells, axis=0))) * lines(mask, 1 - qa, 5)
+            third = third.astype(bf16)
+            blank = jnp.zeros((4 * FEAT, PITCH), bf16)
+            parts.append(jnp.concatenate([third, blank] if qa else [blank, third], axis=1))
+    spread = dot(k3[...].astype(bf16), jnp.concatenate(parts, axis=0))
+
+    def cell(i, j):
+        group = (i + 1) * 6 + j + 1
+        return spread[8 * group : 8 * group + 8]
+
+    def row(i, j):
+        value = lines(cell(i, j), 1, 4)
+        if i == 0:
+            value = value + lines(cell(4, j), 0, 4)
+        if i == 3:
+            value = value + lines(cell(-1, j), 2, 4)
+        return value
+
+    stack = []
+    for i in range(4):
+        cols = [row(i, j) for j in range(-1, 5)]
+        middle = cols[1:5]
+        middle[0] = middle[0] + moved(cols[5], -1)
+        middle[3] = middle[3] + moved(cols[0], 1)
+        stack.append(middle)
+    wide = jnp.concatenate(
+        [jnp.concatenate([lines(stack[i][j], r, 1) for j in range(4)], axis=1) for r in range(4) for i in range(4)], axis=0
+    )
+    source = iota((4 * PITCH, 256), 0)
+    at = source % PITCH - 2
+    target = jnp.where((at >= 0) & (at < COLS), 4 * at + source // PITCH, -1)
+    weave = (iota((4 * PITCH, 256), 1) == target).astype(f32).astype(bf16)
+    high = wide.astype(bf16)
+    low = (wide - high.astype(f32)).astype(bf16)
+    woven = dot(high, weave) + dot(low, weave)
+    for half in range(2):
+        lanes = slice(128 * half, 128 * (half + 1))
+        res[half] = woven[:, lanes]
+        for k in range(3):
+            out[k, :, lanes] = res[half, pl.ds(k, 16, stride=8), :]
+
+
 def last_tile(device):
     return ((device + 1) // 2 + 3) % 4
 
 
 def field_kernel(
-    n_block, n_patch, order, seam, x, w_in, w_mid, w_feat, w_dens, window_out, halo_out, link_out,
+    n_block, n_patch, order, seam, x, w_in, w_mid, w_feat, w_dens, w_conv, w_color, out,
+    window_out, halo_out, k0, k1, k2, k3, res,
     spread, w1, w2, w3, head, rays_out, rays_in, meta, meta_in, depth_rows, tiles, tiles_in, last_in, passed, passed_in,
     halo, halo_in, halo_depth, halo_depth_in, lines16, shares,
     rays_send, rays_recv, meta_send, meta_recv, tile_send, tile_recv, last_send, last_recv, pass_send, pass_recv,
@@ -273,6 +427,8 @@
         @pl.when(mine(unit))
         def _():
             window_out[1 + unit % 2] = passed[unit]
+
+    prepare(w_conv, w_color, k0, k1, k2, k3)
 
     for k in range(1, n_block):
         for copy in halo_copies(k):
@@ -294,7 +450,6 @@
         factor = jnp.where(iota((32, 128), 1) < 64, share[:, 2 * k : 2 * k + 1], share[:, 2 * k + 1 : 2 * k + 2])
         mixed = mixed + factor * tint.astype(f32)
     halo_out[...] = (mixed + pltpu.roll(mixed, 64, 1)).astype(bf16)
-    link_out[...] = meta_in[0, 16:]
 
     for unit in range(3):
 
@@ -312,6 +467,7 @@
             last_copy(k, m).wait_recv()
     mixed = combine(tiles.at[3, last_tile(me)], last_in)
     window_out[me % 2 * 2] = (mixed * jnp.where(me > 0, 1.0, 0.0)).astype(bf16)
+    decode(n_block, n_patch, seam, window_out, halo_out, meta_in.at[0, pl.ds(16, 8)], out, k0, k1, k2, k3, res)
 
     for side in range(2):
         for copy in side_copies(side):
@@ -327,7 +483,7 @@
         pl.when(me % 2 != unit // 2)(more.wait)
 
 
-def field(order, seam, x, w_in, w_mid, w_feat, w_dens, n_block, n_patch):
+def render(order, seam, x, w_in, w_mid, w_feat, w_dens, w_conv, w_color, n_block, n_patch):
     vmem = pl.BlockSpec(memory_space=pltpu.VMEM)
     smem = pl.BlockSpec(memory_space=pltpu.SMEM)
     dma = pltpu.SemaphoreType.DMA
@@ -335,14 +491,17 @@
     rows = 2 * FEAT + 8
     return pl.pallas_call(
         functools.partial(field_kernel, n_block, n_patch),
-        out_shape=[
-            jax.ShapeDtypeStruct((4, FEAT, 128), bf16),
-            jax.ShapeDtypeStruct((32, 128), bf16),
-            jax.ShapeDtypeStruct((8, 128), jnp.int32),
-        ],
-        in_specs=[smem, smem] + [vmem] * 5,
-        out_specs=[vmem] * 3,
+        out_shape=jax.ShapeDtypeStruct((3, 16, 256), f32),
+        in_specs=[smem, smem] + [vmem] * 7,
+        out_specs=vmem,
         scratch_shapes=[
+            pltpu.VMEM((4, FEAT, 128), bf16),
+            pltpu.VMEM((32, 128), bf16),
+            pltpu.VMEM((256, 576), bf16),
+            pltpu.VMEM((256, 1024), bf16),
+            pltpu.VMEM((256, 576), bf16),
+            pltpu.VMEM((288, 1024), f32),
+            pltpu.VMEM((2, 128, 128), f32),
             pltpu.VMEM((128, 1024), bf16),
             pltpu.VMEM((2, 1024, 128), bf16),
             pltpu.VMEM((2, WIDTH, WIDTH), bf16),
@@ -369,184 +528,15 @@
         ],
         compiler_params=pltpu.CompilerParams(collective_id=0, has_side_effects=True),
         name="field",
-    )(order, seam, x, w_in, w_mid, w_feat, w_dens)
-
-
-def phase_source(phase, tap):
-    return (phase + tap - 1) // 2
-
-
-def put(ref, row, col, value):
-    ref[row : row + value.shape[0], col : col + value.shape[1]] = value
-
-
-def enlarge_weights(ref, w_conv, layer):
-    taps = [[w_conv[layer, a, e].astype(f32) for e in range(3)] for a in range(3)]
-    for pa in range(2):
-        for pb in range(2):
-            for dr in range(-1, 2):
-                for dc in range(-1, 2):
-                    hits = [taps[a][e] for a in range(3) for e in range(3)
-                            if phase_source(pa, a) == dr and phase_source(pb, e) == dc]
-                    value = sum(hits[1:], hits[0]) if hits else jnp.zeros((FEAT, FEAT), f32)
-                    put(ref, (2 * pa + pb) * FEAT, ((dr + 1) * 3 + dc + 1) * FEAT, value.astype(bf16))
-
-
-def dense_weights(ref, w_conv, layer):
-    for qa in range(2):
-        for qb in range(2):
-            for s in range(-1, 3):
-                for t in range(-1, 3):
-                    a, e = s - qa + 1, t - qb + 1
-                    inside = 0 <= a <= 2 and 0 <= e <= 2
-                    value = w_conv[layer, a, e] if inside else jnp.zeros((FEAT, FEAT), bf16)
-                    put(ref, (2 * qa + qb) * FEAT, ((s + 1) * 4 + t + 1) * FEAT, value)
-
-
-def colour_weights(ref, w_conv, w_color, layer):
-    ref[...] = jnp.zeros_like(ref)
-    for a in range(3):
-        for e in range(3):
-            tint = dot(w_color[...], w_conv[layer, a, e])
-            for i in range(4):
-                for j in range(4):
-                    group = (i - a + 2) * 6 + (j - e + 2)
-                    cell = ((i // 2 * 2 + j // 2) * 2 + i % 2) * 2 + j % 2
-                    put(ref, 8 * group, cell * FEAT, tint)
-
-
-def moved(x, by):
-    return pltpu.roll(x, (-by) % x.shape[1], 1)
-
-
-def lines(x, first, count):
-    return x[:, first * PITCH : (first + count) * PITCH]
-
-
-def decoder_kernel(n_block, n_patch, seam, window, halo, link, w_conv, w_color, out, k0, k1, k2, k3, res):
-    me = lax.axis_index("block")
-    place = lax.axis_index("patch")
-    enlarge_weights(k0, w_conv, 0)
-    dense_weights(k1, w_conv, 1)
-    enlarge_weights(k2, w_conv, 2)
-    colour_weights(k3, w_conv, w_color, 3)
-
-    lane = iota((1, PITCH), 1)
-    right_open = jnp.where(place < n_patch - 1, seam[0], 0).astype(f32)
-    left_open = link[0:1].astype(f32)
-    inner = jnp.where(lane < 2, left_open, jnp.where(lane < COLS + 2, 1.0, jnp.where(lane < COLS + 4, right_open, 0.0)))
-    top = inner * jnp.where(me > 0, 1.0, 0.0)
-    bottom = inner * jnp.where(me < n_block - 1, 1.0, 0.0)
-    mask = jnp.concatenate([top] + [inner] * 4 + [bottom], axis=1)
-
-    source = iota((128, 256), 0)
-    move = (iota((128, 256), 1) == source // COLS * PITCH + source % COLS + 2).astype(f32).astype(bf16)
-    body = dot(window[...].reshape(4 * FEAT, 128), move)
-    image = jnp.concatenate([body[FEAT * t : FEAT * (t + 1)] for t in range(4)], axis=1)
-    source = iota((32, 8 * PITCH), 0)
-    target = source // 4 * PITCH + source % 2 + source // 2 % 2 * (COLS + 2)
-    halo_move = (iota((32, 8 * PITCH), 1) == target).astype(f32).astype(bf16)
-    image = image + dot(halo[...].astype(f32).T[:FEAT].astype(bf16), halo_move)
-    image = image * jnp.concatenate([inner] * 8, axis=1)
-
-    views = {-1: moved(image, -1).astype(bf16), 0: image.astype(bf16), 1: moved(image, 1).astype(bf16)}
-    patches = jnp.concatenate([lines(views[dc], 1 + dr, 6) for dr in range(-1, 2) for dc in range(-1, 2)], axis=0)
-    first = relu(dot(k0[...], patches)) * mask
-
-    def column_views(maps):
-        cell = lambda a, b: maps[(2 * a + b) * FEAT : (2 * a + b + 1) * FEAT]
-        return [{-1: moved(cell(a, 1), -1).astype(bf16), 0: cell(a, 0).astype(bf16), 1: cell(a, 1).astype(bf16),
-                 2: moved(cell(a, 0), 1).astype(bf16)} for a in range(2)]
-
-    views = column_views(first)
-    empty = jnp.zeros((FEAT, PITCH), bf16)
-    parts = []
-    for s in range(-1, 3):
-        for t in range(-1, 3):
-            view = views[s % 2][t]
-            if s == -1:
-                view = jnp.concatenate([empty, lines(view, 0, 5)], axis=1)
-            if s == 2:
-                view = jnp.concatenate([lines(view, 1, 5), empty], axis=1)
-            parts.append(view)
-    second = relu(dot(k1[...], jnp.concatenate(parts, axis=0))) * mask
-
-    views = column_views(second)
-    parts = []
-    for qa in range(2):
-        for qb in range(2):
-            cells = []
-            for s in range(qa - 1, qa + 2):
-                for t in range(qb - 1, qb + 2):
-                    start = s // 2 + 1 - qa
-                    cells.append(lines(views[s % 2][t], start, 5))
-            third = relu(dot(k2[...], jnp.concatenate(cells, axis=0))) * lines(mask, 1 - qa, 5)
-            third = third.astype(bf16)
-            blank = jnp.zeros((4 * FEAT, PITCH), bf16)
-            parts.append(jnp.concatenate([third, blank] if qa else [blank, third], axis=1))
-    spread = dot(k3[...].astype(bf16), jnp.concatenate(parts, axis=0))
-
-    def cell(i, j):
-        group = (i + 1) * 6 + j + 1
-        return spread[8 * group : 8 * group + 8]
-
-    def row(i, j):
-        value = lines(cell(i, j), 1, 4)
-        if i == 0:
-            value = value + lines(cell(4, j), 0, 4)
-        if i == 3:
-            value = value + lines(cell(-1, j), 2, 4)
-        return value
-
-    stack = []
-    for i in range(4):
-        cols = [row(i, j) for j in range(-1, 5)]
-        middle = cols[1:5]
-        middle[0] = middle[0] + moved(cols[5], -1)
-        middle[3] = middle[3] + moved(cols[0], 1)
-        stack.append(middle)
-    wide = jnp.concatenate(
-        [jnp.concatenate([lines(stack[i][j], r, 1) for j in range(4)], axis=1) for r in range(4) for i in range(4)], axis=0
-    )
-    source = iota((4 * PITCH, 256), 0)
-    at = source % PITCH - 2
-    target = jnp.where((at >= 0) & (at < COLS), 4 * at + source // PITCH, -1)
-    weave = (iota((4 * PITCH, 256), 1) == target).astype(f32).astype(bf16)
-    high = wide.astype(bf16)
-    low = (wide - high.astype(f32)).astype(bf16)
-    woven = dot(high, weave) + dot(low, weave)
-    for half in range(2):
-        lanes = slice(128 * half, 128 * (half + 1))
-        res[half] = woven[:, lanes]
-        for k in range(3):
-            out[k, :, lanes] = res[half, pl.ds(k, 16, stride=8), :]
-
-
-def decoder(seam, window, halo, link, w_conv, w_color, n_block, n_patch):
-    vmem = pl.BlockSpec(memory_space=pltpu.VMEM)
-    return pl.pallas_call(
-        functools.partial(decoder_kernel, n_block, n_patch),
-        out_shape=jax.ShapeDtypeStruct((3, 16, 256), f32),
-        in_specs=[pl.BlockSpec(memory_space=pltpu.SMEM)] + [vmem] * 5,
-        out_specs=vmem,
-        scratch_shapes=[
-            pltpu.VMEM((256, 576), bf16),
-            pltpu.VMEM((256, 1024), bf16),
-            pltpu.VMEM((256, 576), bf16),
-            pltpu.VMEM((288, 1024), f32),
-            pltpu.VMEM((2, 128, 128), f32),
-        ],
-        name="decoder",
-    )(seam, window, halo, link, w_conv, w_color)
+    )(order, seam, x, w_in, w_mid, w_feat, w_dens, w_conv, w_color)
 
 
 def body(samples_in, block_order, seam_link, w_in, w_mid, w_feat, w_density, w_conv, w_color):
     n_block, n_patch = lax.axis_size("block"), lax.axis_size("patch")
     x = samples_in.reshape(2, RAYS // 128, 128, SAMP * ENC)
-    window, halo, link = field(
-        block_order, seam_link, x, w_in, w_mid, jnp.swapaxes(w_feat, 1, 2), w_density, n_block, n_patch
+    return render(
+        block_order, seam_link, x, w_in, w_mid, jnp.swapaxes(w_feat, 1, 2), w_density, w_conv, w_color, n_block, n_patch
     )
-    return decoder(seam_link, window, halo, link, w_conv, w_color, n_block, n_patch)
 
 
 def solution(mesh):

time: 27 us -> 26.7 us (0.989)
  Pallas kernels: 26 us -> 24.4 us
  local copies, waits for them, and re-layouts: 0 us -> 1.42 us
    pallas_call x2 -> x1, Pallas kernels: 26 us -> 24.4 us  [render(): pl.pallas_call(functools.partial(field_kernel, n_block, n_patch), out_sha...]
    unnamed x0 -> x1, local copies, waits for them, and re-layouts: none -> 1.42 us
where the time goes in v5:
time: 26.7 us; the launch traced here: 26.4 us
  Pallas kernels  24.4 us (91%)
  local copies, waits for them, and re-layouts  1.42 us (5%)
  between operations  0.66 us (2%)
    pallas_call x1, Pallas kernels, render(): pl.pallas_call(functools.partial(field_kernel, n_block, n_patch), out_sha...  24.4 us
    unnamed x1, local copies, waits for them, and re-layouts  1.42 us

profile of v5, /device:TPU:225, one launch (start us, length us, event | category | flops | bytes accessed | tf_op | source)
XLA Modules:
  0.0 26.4 jit_solution(160161618230031671)
XLA Ops:
  0.7 24.4 %field.1 = f32[3,16,256]{2,1,0:T(8,128)} custom-call(s32[1,16]{1,0:T(1,128)} %order.1, s32[1]{0:T(128)S(6)} %copy.11.seam, bf16[2,16,128,128]{3,2,1,0:T(8,128)(2,1)} %bitcast.2, bf16[2,32,256]{2,1,0:T(8,128)(2,1)} %w_in.1, bf16[2,2,256,256]{3,2,1,0:T(8,128)(2,1)} %w_mid.1, bf16[2,64,256]{2,1,0:T(8,128)(2,1)} %bitcast.3, bf16[2,256]{1,0:T(2,128)(2,1)} %w_dens.1, ...), custom_call_target="tpu_custom_call" | custom-call | tf_op jit(solution)/shard_map/field/pallas_call | solution.py:492
  25.0 1.4 %copy.12 = f32[3,16,256]{2,1,0:T(8,128)} copy(f32[3,16,256]{2,1,0:T(8,128)} %field.1) | data formatting | bytes 98304

commit v6 on v5

--- a/solution.py
+++ b/solution.py
@@ -300,21 +300,13 @@
         for j in range(4):
             tiles[unit, j, 2 * FEAT :] = rows[:, 128 * j : 128 * (j + 1)]
 
-    def loop(unit, carry):
-        results = field_chunks([(rays_of(unit, m), *weights(m)) for m in range(2)])
+    def store(unit, results):
         for m, (total, tint) in enumerate(results):
             keep(unit, m, tint)
             depth_block(m, total)
         keep_depth(unit)
 
-        @pl.when(unit == 0)
-        def _():
-            count = (place > 0).astype(jnp.int32) + (place < n_patch - 1).astype(jnp.int32)
-            pl.semaphore_wait(barrier, n_block - 1 + count)
-            for side in range(2):
-                for copy in side_copies(side):
-                    pl.when(sides[side][1])(copy.start)
-
+    def send_owner(unit):
         for j in range(4):
             owner = 2 * j + unit // 2
 
@@ -326,14 +318,28 @@
                     device_id=(owner, place), device_id_type=MESH,
                 ).start()
 
-        return carry
-
-    lax.fori_loop(0, 3, loop, 0)
+    results = field_chunks([(rays_of(unit, m), *weights(m)) for unit in range(2) for m in range(2)])
+    store(0, results[:2])
+    store(1, results[2:])
+    count = (place > 0).astype(jnp.int32) + (place < n_patch - 1).astype(jnp.int32)
+    pl.semaphore_wait(barrier, n_block - 1 + count)
+    for side in range(2):
+        for copy in side_copies(side):
+            pl.when(sides[side][1])(copy.start)
+    send_owner(0)
+    send_owner(1)
+    store(2, field_chunks([(rays_of(2, m), *weights(m)) for m in range(2)]))
+    send_owner(2)
 
     for side in range(2):
         for copy in side_copies(side):
             pl.when(sides[1 - side][1])(copy.wait_recv)
-    results = field_chunks([(jnp.concatenate([rays_in[0, m], rays_in[1, m]], axis=0), *weights(m)) for m in range(2)])
+    results = field_chunks(
+        [(jnp.concatenate([rays_in[0, m], rays_in[1, m]], axis=0), *weights(m)) for m in range(2)]
+        + [(rays_of(3, 0), *weights(0))]
+    )
+    ((last_total, last_tint),) = results[2:]
+    results = results[:2]
     for m, (total, tint) in enumerate(results):
         depth_block(m, total)
     halo_depth[...] = depth_rows[:, :128].astype(bf16)
@@ -372,7 +378,7 @@
         )
 
     for m in range(2):
-        ((total, tint),) = field_chunks([(rays_of(3, m), *weights(m))])
+        total, tint = (last_total, last_tint) if m == 0 else field_chunks([(rays_of(3, 1), *weights(1))])[0]
         keep(3, m, tint)
         depth_block(m, total)
         if m == 1:

time: 26.7 us -> 27.8 us (1.041)
  Pallas kernels: 24.4 us -> 25.6 us
    pallas_call x1, Pallas kernels: 24.4 us -> 25.6 us  [render(): pl.pallas_call(functools.partial(field_kernel, n_block, n_patch), out_sha...]
where the time goes in v6:
time: 27.8 us; the launch traced here: 27.6 us
  Pallas kernels  25.6 us (92%)
  local copies, waits for them, and re-layouts  1.42 us (5%)
  between operations  0.66 us (2%)
    pallas_call x1, Pallas kernels, render(): pl.pallas_call(functools.partial(field_kernel, n_block, n_patch), out_sha...  25.6 us
    unnamed x1, local copies, waits for them, and re-layouts  1.42 us

profile of v6, /device:TPU:225, one launch (start us, length us, event | category | flops | bytes accessed | tf_op | source)
XLA Modules:
  0.0 27.6 jit_solution(7306051994860846283)
XLA Ops:
  0.7 25.6 %field.1 = f32[3,16,256]{2,1,0:T(8,128)} custom-call(s32[1,16]{1,0:T(1,128)} %order.1, s32[1]{0:T(128)S(6)} %copy.11.seam, bf16[2,16,128,128]{3,2,1,0:T(8,128)(2,1)} %bitcast.2, bf16[2,32,256]{2,1,0:T(8,128)(2,1)} %w_in.1, bf16[2,2,256,256]{3,2,1,0:T(8,128)(2,1)} %w_mid.1, bf16[2,64,256]{2,1,0:T(8,128)(2,1)} %bitcast.3, bf16[2,256]{1,0:T(2,128)(2,1)} %w_dens.1, ...), custom_call_target="tpu_custom_call" | custom-call | tf_op jit(solution)/shard_map/field/pallas_call | solution.py:498
  26.2 1.4 %copy.12 = f32[3,16,256]{2,1,0:T(8,128)} copy(f32[3,16,256]{2,1,0:T(8,128)} %field.1) | data formatting | bytes 98304

commit v7 on v6

--- a/solution.py
+++ b/solution.py
@@ -17,7 +17,9 @@
 WIDTH = 256
 COLS = 64
 RAYS = 2048
-PITCH = 128
+PITCH = 68
+SPAN = 512
+ROLL = bf16
 
 
 def iota(shape, dim):
@@ -103,89 +105,76 @@
 
 
 def moved(x, by):
-    return pltpu.roll(x, (-by) % x.shape[1], 1)
-
-
-def lines(x, first, count):
-    return x[:, first * PITCH : (first + count) * PITCH]
-
-
-def prepare(w_conv, w_color, k0, k1, k2, k3):
+    return pltpu.roll(x, (-by) % x.shape[1], 1) if by else x
+
+
+def prepare(w_conv, w_color, k0, k1, k2, k3, k4, place, halo_place, weave):
     enlarge_weights(k0, w_conv, 0)
     dense_weights(k1, w_conv, 1)
     enlarge_weights(k2, w_conv, 2)
     colour_weights(k3, w_conv, w_color, 3)
-
-
-def decode(n_block, n_patch, seam, window, halo, link, out, k0, k1, k2, k3, res):
+    k4[...] = k3[...].astype(bf16)
+    source = iota(place.shape, 0)
+    place[...] = (iota(place.shape, 1) == source // COLS * PITCH + source % COLS + 2).astype(f32).astype(bf16)
+    source = iota(halo_place.shape, 0)
+    target = source // 4 * PITCH + source % 2 + source // 2 % 2 * (COLS + 2)
+    halo_place[...] = (iota(halo_place.shape, 1) == target).astype(f32).astype(bf16)
+    source = iota(weave.shape, 0)
+    target = jnp.where(source % 128 < COLS, 4 * (source % 128) + source // 128, -1)
+    weave[...] = (iota(weave.shape, 1) == target).astype(f32).astype(bf16)
+
+
+def decode(n_block, n_patch, seam, window, halo, link, out, k0, k1, k2, k4, place, halo_place, weave, res):
     me = lax.axis_index("block")
-    place = lax.axis_index("patch")
-
-    lane = iota((1, PITCH), 1)
-    right_open = jnp.where(place < n_patch - 1, seam[0], 0).astype(f32)
-    left_open = link[0:1].astype(f32)
-    inner = jnp.where(lane < 2, left_open, jnp.where(lane < COLS + 2, 1.0, jnp.where(lane < COLS + 4, right_open, 0.0)))
-    top = inner * jnp.where(me > 0, 1.0, 0.0)
-    bottom = inner * jnp.where(me < n_block - 1, 1.0, 0.0)
-    mask = jnp.concatenate([top] + [inner] * 4 + [bottom], axis=1)
-
-    source = iota((128, 256), 0)
-    move = (iota((128, 256), 1) == source // COLS * PITCH + source % COLS + 2).astype(f32).astype(bf16)
-    body = dot(window[...].reshape(4 * FEAT, 128), move)
-    image = jnp.concatenate([body[FEAT * t : FEAT * (t + 1)] for t in range(4)], axis=1)
-    source = iota((32, 8 * PITCH), 0)
-    target = source // 4 * PITCH + source % 2 + source // 2 % 2 * (COLS + 2)
-    halo_move = (iota((32, 8 * PITCH), 1) == target).astype(f32).astype(bf16)
-    image = image + dot(halo[...].astype(f32).T[:FEAT].astype(bf16), halo_move)
-    image = image * jnp.concatenate([inner] * 8, axis=1)
-
-    views = {-1: moved(image, -1).astype(bf16), 0: image.astype(bf16), 1: moved(image, 1).astype(bf16)}
-    patches = jnp.concatenate([lines(views[dc], 1 + dr, 6) for dr in range(-1, 2) for dc in range(-1, 2)], axis=0)
-    first = relu(dot(k0[...], patches)) * mask
-
-    def column_views(maps):
-        cell = lambda a, b: maps[(2 * a + b) * FEAT : (2 * a + b + 1) * FEAT]
-        return [{-1: moved(cell(a, 1), -1).astype(bf16), 0: cell(a, 0).astype(bf16), 1: cell(a, 1).astype(bf16),
-                 2: moved(cell(a, 0), 1).astype(bf16)} for a in range(2)]
-
-    views = column_views(first)
-    empty = jnp.zeros((FEAT, PITCH), bf16)
-    parts = []
-    for s in range(-1, 3):
-        for t in range(-1, 3):
-            view = views[s % 2][t]
-            if s == -1:
-                view = jnp.concatenate([empty, lines(view, 0, 5)], axis=1)
-            if s == 2:
-                view = jnp.concatenate([lines(view, 1, 5), empty], axis=1)
-            parts.append(view)
-    second = relu(dot(k1[...], jnp.concatenate(parts, axis=0))) * mask
-
-    views = column_views(second)
+    column = lax.axis_index("patch")
+    right_open = jnp.where(column < n_patch - 1, seam[0], 0).astype(f32)
+    left_open = link[0:1, 0:1].astype(f32)
+
+    def open_sides(lanes):
+        at = iota((1, lanes), 1) % PITCH
+        return jnp.where(at < 2, left_open, jnp.where(at < COLS + 2, 1.0, right_open))
+
+    line = iota((1, SPAN), 1) // PITCH
+    top = jnp.where(me > 0, 1.0, 0.0)
+    bottom = jnp.where(me < n_block - 1, 1.0, 0.0)
+    mask = jnp.where(line == 0, top, jnp.where(line < 5, 1.0, jnp.where(line == 5, bottom, 0.0))) * open_sides(SPAN)
+
+    image = dot(jnp.concatenate([window[t] for t in range(4)], axis=1), place[...])
+    image = image + dot(halo[...].astype(f32).T[:FEAT].astype(bf16), halo_place[...])
+    image = (image * open_sides(image.shape[1])).astype(ROLL)
+    patches = [
+        moved(image, (dr + 1) * PITCH + dc)[:, :SPAN].astype(bf16) for dr in range(-1, 2) for dc in range(-1, 2)
+    ]
+    first = (relu(dot(k0[...], jnp.concatenate(patches, axis=0))) * mask).astype(ROLL)
+
+    def views(maps):
+        found = {}
+        for s in range(-1, 3):
+            for t in range(-1, 3):
+                phase = (s % 2 * 2 + t % 2) * FEAT
+                found[s, t] = moved(maps[phase : phase + FEAT], s // 2 * PITCH + t // 2).astype(bf16)
+        return found
+
+    cells = views(first)
+    second = relu(dot(k1[...], jnp.concatenate([cells[s, t] for s in range(-1, 3) for t in range(-1, 3)], axis=0)))
+    cells = views((second * mask).astype(ROLL))
     parts = []
     for qa in range(2):
         for qb in range(2):
-            cells = []
-            for s in range(qa - 1, qa + 2):
-                for t in range(qb - 1, qb + 2):
-                    start = s // 2 + 1 - qa
-                    cells.append(lines(views[s % 2][t], start, 5))
-            third = relu(dot(k2[...], jnp.concatenate(cells, axis=0))) * lines(mask, 1 - qa, 5)
-            third = third.astype(bf16)
-            blank = jnp.zeros((4 * FEAT, PITCH), bf16)
-            parts.append(jnp.concatenate([third, blank] if qa else [blank, third], axis=1))
-    spread = dot(k3[...].astype(bf16), jnp.concatenate(parts, axis=0))
+            near = [cells[s, t] for s in range(qa - 1, qa + 2) for t in range(qb - 1, qb + 2)]
+            parts.append((relu(dot(k2[...], jnp.concatenate(near, axis=0))) * mask).astype(bf16))
+    spread = dot(k4[...], jnp.concatenate(parts, axis=0))
 
     def cell(i, j):
         group = (i + 1) * 6 + j + 1
         return spread[8 * group : 8 * group + 8]
 
     def row(i, j):
-        value = lines(cell(i, j), 1, 4)
+        value = cell(i, j)
         if i == 0:
-            value = value + lines(cell(4, j), 0, 4)
+            value = value + moved(cell(4, j), -PITCH)
         if i == 3:
-            value = value + lines(cell(-1, j), 2, 4)
+            value = value + moved(cell(-1, j), PITCH)
         return value
 
     stack = []
@@ -194,17 +183,21 @@
         middle = cols[1:5]
         middle[0] = middle[0] + moved(cols[5], -1)
         middle[3] = middle[3] + moved(cols[0], 1)
-        stack.append(middle)
+        stack.append(jnp.concatenate(middle, axis=0))
+    stack = jnp.concatenate(stack, axis=0)
+    starts = [(r + 1) * PITCH + 2 for r in range(4)]
+    lines = [moved(stack[:, a // 128 * 128 : a // 128 * 128 + 256], a % 128)[:, :128] for a in starts[:3]]
+    lines.append(moved(stack, starts[3])[:, :128])
     wide = jnp.concatenate(
-        [jnp.concatenate([lines(stack[i][j], r, 1) for j in range(4)], axis=1) for r in range(4) for i in range(4)], axis=0
+        [
+            jnp.concatenate([lines[r][8 * (4 * i + j) : 8 * (4 * i + j) + 8] for j in range(4)], axis=1)
+            for r in range(4) for i in range(4)
+        ],
+        axis=0,
     )
-    source = iota((4 * PITCH, 256), 0)
-    at = source % PITCH - 2
-    target = jnp.where((at >= 0) & (at < COLS), 4 * at + source // PITCH, -1)
-    weave = (iota((4 * PITCH, 256), 1) == target).astype(f32).astype(bf16)
     high = wide.astype(bf16)
     low = (wide - high.astype(f32)).astype(bf16)
-    woven = dot(high, weave) + dot(low, weave)
+    woven = dot(high, weave[...]) + dot(low, weave[...])
     for half in range(2):
         lanes = slice(128 * half, 128 * (half + 1))
         res[half] = woven[:, lanes]
@@ -217,8 +210,9 @@
 
 
 def field_kernel(
-    n_block, n_patch, order, seam, x, w_in, w_mid, w_feat, w_dens, w_conv, w_color, out,
-    window_out, halo_out, k0, k1, k2, k3, res,
+    n_block, n_patch, seam, order_far, x_far, w_in_far, w_mid_far, w_feat_far, w_dens_far, w_conv_far, w_color_far, out,
+    order, x, w_in, w_mid, w_feat, w_dens, w_conv, w_color, fetched,
+    window_out, halo_out, k0, k1, k2, k3, k4, place_rows, place_halo, weave, res,
     spread, w1, w2, w3, head, rays_out, rays_in, meta, meta_in, depth_rows, tiles, tiles_in, last_in, passed, passed_in,
     halo, halo_in, halo_depth, halo_depth_in, lines16, shares,
     rays_send, rays_recv, meta_send, meta_recv, tile_send, tile_recv, last_send, last_recv, pass_send, pass_recv,
@@ -227,6 +221,13 @@
     me = lax.axis_index("block")
     place = lax.axis_index("patch")
     sides = ((place - 1, place > 0), (place + 1, place < n_patch - 1))
+    pairs = (
+        (w_in_far, w_in), (w_mid_far, w_mid), (w_feat_far, w_feat), (w_dens_far, w_dens), (x_far, x), (order_far, order),
+        (w_conv_far, w_conv), (w_color_far, w_color),
+    )
+    fetches = [pltpu.make_async_copy(far, near, fetched.at[i]) for i, (far, near) in enumerate(pairs)]
+    for fetch in fetches:
+        fetch.start()
     rays_in[...] = jnp.zeros_like(rays_in)
     meta_in[...] = jnp.zeros_like(meta_in)
     barrier = pltpu.get_barrier_semaphore()
@@ -238,6 +239,19 @@
         def _():
             pl.semaphore_signal(barrier, inc=1, device_id=(me, side), device_id_type=MESH)
 
+    spread[...] = jnp.zeros_like(spread)
+    for fetch in fetches[:4]:
+        fetch.wait()
+    for m in range(2):
+        for s in range(SAMP):
+            spread[ENC * s : ENC * (s + 1), WIDTH * s : WIDTH * (s + 1)] = w_in[m]
+        w1[m] = spread[...].T
+        w2[m] = w_mid[m, 0].T
+        w3[m] = w_mid[m, 1].T
+        head[m, :FEAT] = w_feat[m]
+        head[m, FEAT:] = jnp.broadcast_to(w_dens[pl.ds(m, 1), :], (16, WIDTH))
+    for fetch in fetches[4:6]:
+        fetch.wait()
     line = iota((16, 256), 0)
     wanted = line % 8 // 2 * COLS + line % 2 + jnp.where(line >= 8, COLS - 2, 0)
     pick = (iota((16, 256), 1) == wanted).astype(f32).astype(bf16)
@@ -254,15 +268,6 @@
     meta[:16] = rank
     meta[16:] = jnp.full((8, 128), jnp.where(place < n_patch - 1, seam[0], 0), jnp.int32)
 
-    spread[...] = jnp.zeros_like(spread)
-    for m in range(2):
-        for s in range(SAMP):
-            spread[ENC * s : ENC * (s + 1), WIDTH * s : WIDTH * (s + 1)] = w_in[m]
-        w1[m] = spread[...].T
-        w2[m] = w_mid[m, 0].T
-        w3[m] = w_mid[m, 1].T
-        head[m, :FEAT] = w_feat[m]
-        head[m, FEAT:] = jnp.broadcast_to(w_dens[pl.ds(m, 1), :], (16, WIDTH))
     depth_rows[...] = jnp.zeros_like(depth_rows)
 
     def side_copies(side):
@@ -278,6 +283,12 @@
             ),
         ]
 
+    count = (place > 0).astype(jnp.int32) + (place < n_patch - 1).astype(jnp.int32)
+    pl.semaphore_wait(barrier, n_block - 1 + count)
+    for side in range(2):
+        for copy in side_copies(side):
+            pl.when(sides[side][1])(copy.start)
+
     def weights(m):
         return w1[m], w2[m], w3[m], head[m]
 
@@ -321,11 +332,6 @@
     results = field_chunks([(rays_of(unit, m), *weights(m)) for unit in range(2) for m in range(2)])
     store(0, results[:2])
     store(1, results[2:])
-    count = (place > 0).astype(jnp.int32) + (place < n_patch - 1).astype(jnp.int32)
-    pl.semaphore_wait(barrier, n_block - 1 + count)
-    for side in range(2):
-        for copy in side_copies(side):
-            pl.when(sides[side][1])(copy.start)
     send_owner(0)
     send_owner(1)
     store(2, field_chunks([(rays_of(2, m), *weights(m)) for m in range(2)]))
@@ -434,7 +440,9 @@
         def _():
             window_out[1 + unit % 2] = passed[unit]
 
-    prepare(w_conv, w_color, k0, k1, k2, k3)
+    for fetch in fetches[6:]:
+        fetch.wait()
+    prepare(w_conv, w_color, k0, k1, k2, k3, k4, place_rows, place_halo, weave)
 
     for k in range(1, n_block):
         for copy in halo_copies(k):
@@ -473,7 +481,10 @@
             last_copy(k, m).wait_recv()
     mixed = combine(tiles.at[3, last_tile(me)], last_in)
     window_out[me % 2 * 2] = (mixed * jnp.where(me > 0, 1.0, 0.0)).astype(bf16)
-    decode(n_block, n_patch, seam, window_out, halo_out, meta_in.at[0, pl.ds(16, 8)], out, k0, k1, k2, k3, res)
+    decode(
+        n_block, n_patch, seam, window_out, halo_out, meta_in.at[0, pl.ds(16, 8)], out, k0, k1, k2, k4,
+        place_rows, place_halo, weave, res,
+    )
 
     for side in range(2):
         for copy in side_copies(side):
@@ -498,15 +509,22 @@
     return pl.pallas_call(
         functools.partial(field_kernel, n_block, n_patch),
         out_shape=jax.ShapeDtypeStruct((3, 16, 256), f32),
-        in_specs=[smem, smem] + [vmem] * 7,
+        in_specs=[smem] + [pl.BlockSpec(memory_space=pl.ANY)] * 8,
         out_specs=vmem,
         scratch_shapes=[
+            pltpu.SMEM(order.shape, jnp.int32),
+            *[pltpu.VMEM(array.shape, bf16) for array in (x, w_in, w_mid, w_feat, w_dens, w_conv, w_color)],
+            dma((8,)),
             pltpu.VMEM((4, FEAT, 128), bf16),
             pltpu.VMEM((32, 128), bf16),
             pltpu.VMEM((256, 576), bf16),
             pltpu.VMEM((256, 1024), bf16),
             pltpu.VMEM((256, 576), bf16),
             pltpu.VMEM((288, 1024), f32),
+            pltpu.VMEM((288, 1024), bf16),
+            pltpu.VMEM((512, 640), bf16),
+            pltpu.VMEM((32, 640), bf16),
+            pltpu.VMEM((512, 256), bf16),
             pltpu.VMEM((2, 128, 128), f32),
             pltpu.VMEM((128, 1024), bf16),
             pltpu.VMEM((2, 1024, 128), bf16),
@@ -534,7 +552,7 @@
         ],
         compiler_params=pltpu.CompilerParams(collective_id=0, has_side_effects=True),
         name="field",
-    )(order, seam, x, w_in, w_mid, w_feat, w_dens, w_conv, w_color)
+    )(seam, order, x, w_in, w_mid, w_feat, w_dens, w_conv, w_color)
 
 
 def body(samples_in, block_order, seam_link, w_in, w_mid, w_feat, w_density, w_conv, w_color):

time: 27.8 us -> 26.7 us (0.960)
  Pallas kernels: 25.6 us -> 24.3 us
    pallas_call x1, Pallas kernels: 25.6 us -> 24.3 us  [render(): pl.pallas_call(functools.partial(field_kernel, n_block, n_patch), out_sha...]
where the time goes in v7:
time: 26.7 us; the launch traced here: 26.3 us
  Pallas kernels  24.3 us (91%)
  local copies, waits for them, and re-layouts  1.42 us (5%)
  between operations  0.66 us (2%)
    pallas_call x1, Pallas kernels, render(): pl.pallas_call(functools.partial(field_kernel, n_block, n_patch), out_sha...  24.3 us
    unnamed x1, local copies, waits for them, and re-layouts  1.42 us

profile of v7, /device:TPU:225, one launch (start us, length us, event | category | flops | bytes accessed | tf_op | source)
XLA Modules:
  0.0 26.3 jit_solution(594881300000081269)
XLA Ops:
  0.7 24.3 %field.1 = f32[3,16,256]{2,1,0:T(8,128)} custom-call(s32[1]{0:T(128)S(6)} %copy.11.seam, s32[1,16]{1,0:T(1,128)} %order_far.1, bf16[2,16,128,128]{3,2,1,0:T(8,128)(2,1)} %bitcast.2, bf16[2,32,256]{2,1,0:T(8,128)(2,1)} %w_in_far.1, bf16[2,2,256,256]{3,2,1,0:T(8,128)(2,1)} %w_mid_far.1, bf16[2,64,256]{2,1,0:T(8,128)(2,1)} %bitcast.3, ...), custom_call_target="tpu_custom_call" | custom-call | tf_op jit(solution)/shard_map/field/pallas_call | solution.py:509
  24.9 1.4 %copy.12 = f32[3,16,256]{2,1,0:T(8,128)} copy(f32[3,16,256]{2,1,0:T(8,128)} %field.1) | data formatting | bytes 98304

commit v8 on v7

--- a/solution.py
+++ b/solution.py
@@ -329,13 +329,12 @@
                     device_id=(owner, place), device_id_type=MESH,
                 ).start()
 
-    results = field_chunks([(rays_of(unit, m), *weights(m)) for unit in range(2) for m in range(2)])
-    store(0, results[:2])
-    store(1, results[2:])
-    send_owner(0)
-    send_owner(1)
-    store(2, field_chunks([(rays_of(2, m), *weights(m)) for m in range(2)]))
-    send_owner(2)
+    def loop(unit, carry):
+        store(unit, field_chunks([(rays_of(unit, m), *weights(m)) for m in range(2)]))
+        send_owner(unit)
+        return carry
+
+    lax.fori_loop(0, 3, loop, 0)
 
     for side in range(2):
         for copy in side_copies(side):

time: 26.7 us -> 26.3 us (0.985)
  no operation moved by 1% of the time
where the time goes in v8:
time: 26.3 us; the launch traced here: 26.2 us
  Pallas kernels  24.1 us (92%)
  local copies, waits for them, and re-layouts  1.42 us (5%)
  between operations  0.66 us (3%)
    pallas_call x1, Pallas kernels, render(): pl.pallas_call(functools.partial(field_kernel, n_block, n_patch), out_sha...  24.1 us
    unnamed x1, local copies, waits for them, and re-layouts  1.42 us

profile of v8, /device:TPU:225, one launch (start us, length us, event | category | flops | bytes accessed | tf_op | source)
XLA Modules:
  0.0 26.2 jit_solution(17084586532969742150)
XLA Ops:
  0.7 24.1 %field.1 = f32[3,16,256]{2,1,0:T(8,128)} custom-call(s32[1]{0:T(128)S(6)} %copy.11.seam, s32[1,16]{1,0:T(1,128)} %order_far.1, bf16[2,16,128,128]{3,2,1,0:T(8,128)(2,1)} %bitcast.2, bf16[2,32,256]{2,1,0:T(8,128)(2,1)} %w_in_far.1, bf16[2,2,256,256]{3,2,1,0:T(8,128)(2,1)} %w_mid_far.1, bf16[2,64,256]{2,1,0:T(8,128)(2,1)} %bitcast.3, ...), custom_call_target="tpu_custom_call" | custom-call | tf_op jit(solution)/shard_map/field/pallas_call | solution.py:508
  24.7 1.4 %copy.12 = f32[3,16,256]{2,1,0:T(8,128)} copy(f32[3,16,256]{2,1,0:T(8,128)} %field.1) | data formatting | bytes 98304

commit v9 on v8

--- a/solution.py
+++ b/solution.py
@@ -220,6 +220,7 @@
 ):
     me = lax.axis_index("block")
     place = lax.axis_index("patch")
+    far_first = sorted(range(1, n_block), key=lambda k: abs(k - n_block // 2))
     sides = ((place - 1, place > 0), (place + 1, place < n_patch - 1))
     pairs = (
         (w_in_far, w_in), (w_mid_far, w_mid), (w_feat_far, w_feat), (w_dens_far, w_dens), (x_far, x), (order_far, order),
@@ -369,7 +370,7 @@
             ),
         ]
 
-    for k in range(1, n_block):
+    for k in far_first:
         for copy in halo_copies(k):
             copy.start()
 
@@ -388,7 +389,7 @@
         depth_block(m, total)
         if m == 1:
             keep_depth(3)
-        for k in range(1, n_block):
+        for k in far_first:
             last_copy(k, m).start()
 
     def order_weights(blocks, ranks):
@@ -507,7 +508,7 @@
     rows = 2 * FEAT + 8
     return pl.pallas_call(
         functools.partial(field_kernel, n_block, n_patch),
-        out_shape=jax.ShapeDtypeStruct((3, 16, 256), f32),
+        out_shape=pltpu.VMEM((3, 16, 256), f32),
         in_specs=[smem] + [pl.BlockSpec(memory_space=pl.ANY)] * 8,
         out_specs=vmem,
         scratch_shapes=[

time: 26.3 us -> 24.6 us (0.935)
  Pallas kernels: 24.1 us -> 23.2 us
  local copies, waits for them, and re-layouts: 1.42 us -> 0.62 us
    pallas_call x1, Pallas kernels: 24.1 us -> 23.2 us  [render(): pl.pallas_call(functools.partial(field_kernel, n_block, n_patch), out_sha...]
    unnamed x1, local copies, waits for them, and re-layouts: 1.42 us -> 0.62 us
where the time goes in v9:
time: 24.6 us; the launch traced here: 24.5 us
  Pallas kernels  23.2 us (94%)
  between operations  0.66 us (3%)
  local copies, waits for them, and re-layouts  0.62 us (3%)
    pallas_call x1, Pallas kernels, render(): pl.pallas_call(functools.partial(field_kernel, n_block, n_patch), out_sha...  23.2 us
    unnamed x1, local copies, waits for them, and re-layouts  0.62 us

profile of v9, /device:TPU:225, one launch (start us, length us, event | category | flops | bytes accessed | tf_op | source)
XLA Modules:
  0.0 24.5 jit_solution(1031654494522229240)
XLA Ops:
  0.7 23.2 %field.1 = f32[3,16,256]{2,1,0:T(8,128)S(1)} custom-call(s32[1]{0:T(128)S(6)} %copy.12.seam, s32[1,16]{1,0:T(1,128)} %order_far.1, bf16[2,16,128,128]{3,2,1,0:T(8,128)(2,1)} %bitcast.2, bf16[2,32,256]{2,1,0:T(8,128)(2,1)} %w_in_far.1, bf16[2,2,256,256]{3,2,1,0:T(8,128)(2,1)} %w_mid_far.1, bf16[2,64,256]{2,1,0:T(8,128)(2,1)} %bitcast.3, ...), custom_call_target="tpu_custom_call" | custom-call | tf_op jit(solution)/shard_map/field/pallas_call | solution.py:509
  23.8 0.6 %copy.11 = f32[3,16,256]{2,1,0:T(8,128)} copy(f32[3,16,256]{2,1,0:T(8,128)S(1)} %field.1) | data formatting | bytes 98304

commit v10 on v9

--- a/solution.py
+++ b/solution.py
@@ -81,6 +81,17 @@
                     put(ref, (2 * pa + pb) * FEAT, ((dr + 1) * 3 + dc + 1) * FEAT, value.astype(bf16))
 
 
+def window_weights(ref, w_conv, layer):
+    taps = [[w_conv[layer, a, e].astype(f32) for e in range(3)] for a in range(3)]
+    for ua in range(2):
+        for ub in range(2):
+            for da in range(2):
+                for db in range(2):
+                    hits = [taps[a][e] for a in range(3) for e in range(3)
+                            if phase_source(ua, a) == ua - 1 + da and phase_source(ub, e) == ub - 1 + db]
+                    put(ref.at[2 * ua + ub], 0, (2 * da + db) * FEAT, sum(hits[1:], hits[0]).astype(bf16))
+
+
 def dense_weights(ref, w_conv, layer):
     for qa in range(2):
         for qb in range(2):
@@ -111,7 +122,7 @@
 def prepare(w_conv, w_color, k0, k1, k2, k3, k4, place, halo_place, weave):
     enlarge_weights(k0, w_conv, 0)
     dense_weights(k1, w_conv, 1)
-    enlarge_weights(k2, w_conv, 2)
+    window_weights(k2, w_conv, 2)
     colour_weights(k3, w_conv, w_color, 3)
     k4[...] = k3[...].astype(bf16)
     source = iota(place.shape, 0)
@@ -158,11 +169,16 @@
     cells = views(first)
     second = relu(dot(k1[...], jnp.concatenate([cells[s, t] for s in range(-1, 3) for t in range(-1, 3)], axis=0)))
     cells = views((second * mask).astype(ROLL))
-    parts = []
-    for qa in range(2):
-        for qb in range(2):
-            near = [cells[s, t] for s in range(qa - 1, qa + 2) for t in range(qb - 1, qb + 2)]
-            parts.append((relu(dot(k2[...], jnp.concatenate(near, axis=0))) * mask).astype(bf16))
+    third = {}
+    for wa in range(3):
+        for wb in range(3):
+            near = [cells[wa - 1 + da, wb - 1 + db] for da in range(2) for db in range(2)]
+            users = [(ua, ub) for ua in range(2) for ub in range(2) if 0 <= wa - ua <= 1 and 0 <= wb - ub <= 1]
+            kernels = jnp.concatenate([k2[2 * ua + ub] for ua, ub in users], axis=0)
+            found = (relu(dot(kernels, jnp.concatenate(near, axis=0))) * mask).astype(bf16)
+            for i, (ua, ub) in enumerate(users):
+                third[wa - ua, wb - ub, ua, ub] = found[FEAT * i : FEAT * (i + 1)]
+    parts = [third[key] for key in sorted(third)]
     spread = dot(k4[...], jnp.concatenate(parts, axis=0))
 
     def cell(i, j):
@@ -519,7 +535,7 @@
             pltpu.VMEM((32, 128), bf16),
             pltpu.VMEM((256, 576), bf16),
             pltpu.VMEM((256, 1024), bf16),
-            pltpu.VMEM((256, 576), bf16),
+            pltpu.VMEM((4, FEAT, 256), bf16),
             pltpu.VMEM((288, 1024), f32),
             pltpu.VMEM((288, 1024), bf16),
             pltpu.VMEM((512, 640), bf16),

time: 24.6 us -> 24.2 us (0.984)
  Pallas kernels: 23.2 us -> 22.8 us
    pallas_call x1, Pallas kernels: 23.2 us -> 22.8 us  [render(): pl.pallas_call(functools.partial(field_kernel, n_block, n_patch), out_sha...]
where the time goes in v10:
time: 24.2 us; the launch traced here: 24 us
  Pallas kernels  22.8 us (94%)
  between operations  0.66 us (3%)
  local copies, waits for them, and re-layouts  0.62 us (3%)
    pallas_call x1, Pallas kernels, render(): pl.pallas_call(functools.partial(field_kernel, n_block, n_patch), out_sha...  22.8 us
    unnamed x1, local copies, waits for them, and re-layouts  0.62 us

profile of v10, /device:TPU:225, one launch (start us, length us, event | category | flops | bytes accessed | tf_op | source)
XLA Modules:
  0.0 24.0 jit_solution(14812654473594458128)
XLA Ops:
  0.7 22.8 %field.1 = f32[3,16,256]{2,1,0:T(8,128)S(1)} custom-call(s32[1]{0:T(128)S(6)} %copy.12.seam, s32[1,16]{1,0:T(1,128)} %order_far.1, bf16[2,16,128,128]{3,2,1,0:T(8,128)(2,1)} %bitcast.2, bf16[2,32,256]{2,1,0:T(8,128)(2,1)} %w_in_far.1, bf16[2,2,256,256]{3,2,1,0:T(8,128)(2,1)} %w_mid_far.1, bf16[2,64,256]{2,1,0:T(8,128)(2,1)} %bitcast.3, ...), custom_call_target="tpu_custom_call" | custom-call | tf_op jit(solution)/shard_map/field/pallas_call | solution.py:525
  23.4 0.6 %copy.11 = f32[3,16,256]{2,1,0:T(8,128)} copy(f32[3,16,256]{2,1,0:T(8,128)S(1)} %field.1) | data formatting | bytes 98304

commit v11 on v10

--- a/solution.py
+++ b/solution.py
@@ -351,17 +351,18 @@
         send_owner(unit)
         return carry
 
-    lax.fori_loop(0, 3, loop, 0)
+    lax.fori_loop(0, 2, loop, 0)
 
     for side in range(2):
         for copy in side_copies(side):
             pl.when(sides[1 - side][1])(copy.wait_recv)
     results = field_chunks(
-        [(jnp.concatenate([rays_in[0, m], rays_in[1, m]], axis=0), *weights(m)) for m in range(2)]
-        + [(rays_of(3, 0), *weights(0))]
+        [(rays_of(2, m), *weights(m)) for m in range(2)]
+        + [(jnp.concatenate([rays_in[0, m], rays_in[1, m]], axis=0), *weights(m)) for m in range(2)]
     )
-    ((last_total, last_tint),) = results[2:]
-    results = results[:2]
+    store(2, results[:2])
+    send_owner(2)
+    results = results[2:]
     for m, (total, tint) in enumerate(results):
         depth_block(m, total)
     halo_depth[...] = depth_rows[:, :128].astype(bf16)
@@ -400,7 +401,7 @@
         )
 
     for m in range(2):
-        total, tint = (last_total, last_tint) if m == 0 else field_chunks([(rays_of(3, 1), *weights(1))])[0]
+        ((total, tint),) = field_chunks([(rays_of(3, m), *weights(m))])
         keep(3, m, tint)
         depth_block(m, total)
         if m == 1:

time: 24.2 us -> 24.4 us (level)
  no operation moved by 1% of the time
where the time goes in v11:
time: 24.4 us; the launch traced here: 24.1 us
  Pallas kernels  22.8 us (93%)
  between operations  0.66 us (3%)
  local copies, waits for them, and re-layouts  0.62 us (3%)
    pallas_call x1, Pallas kernels, render(): pl.pallas_call(functools.partial(field_kernel, n_block, n_patch), out_sha...  22.8 us
    unnamed x1, local copies, waits for them, and re-layouts  0.62 us

profile of v11, /device:TPU:225, one launch (start us, length us, event | category | flops | bytes accessed | tf_op | source)
XLA Modules:
  0.0 24.1 jit_solution(13014372836689649513)
XLA Ops:
  0.7 22.8 %field.1 = f32[3,16,256]{2,1,0:T(8,128)S(1)} custom-call(s32[1]{0:T(128)S(6)} %copy.12.seam, s32[1,16]{1,0:T(1,128)} %order_far.1, bf16[2,16,128,128]{3,2,1,0:T(8,128)(2,1)} %bitcast.2, bf16[2,32,256]{2,1,0:T(8,128)(2,1)} %w_in_far.1, bf16[2,2,256,256]{3,2,1,0:T(8,128)(2,1)} %w_mid_far.1, bf16[2,64,256]{2,1,0:T(8,128)(2,1)} %bitcast.3, ...), custom_call_target="tpu_custom_call" | custom-call | tf_op jit(solution)/shard_map/field/pallas_call | solution.py:526
  23.5 0.6 %copy.11 = f32[3,16,256]{2,1,0:T(8,128)} copy(f32[3,16,256]{2,1,0:T(8,128)S(1)} %field.1) | data formatting | bytes 98304

commit v12 on v11

--- a/solution.py
+++ b/solution.py
@@ -493,16 +493,6 @@
     def _():
         window_out[3] = jnp.zeros((FEAT, 128), bf16)
 
-    for m in range(2):
-        for k in range(1, n_block):
-            last_copy(k, m).wait_recv()
-    mixed = combine(tiles.at[3, last_tile(me)], last_in)
-    window_out[me % 2 * 2] = (mixed * jnp.where(me > 0, 1.0, 0.0)).astype(bf16)
-    decode(
-        n_block, n_patch, seam, window_out, halo_out, meta_in.at[0, pl.ds(16, 8)], out, k0, k1, k2, k4,
-        place_rows, place_halo, weave, res,
-    )
-
     for side in range(2):
         for copy in side_copies(side):
             pl.when(sides[side][1])(copy.wait_send)
@@ -515,6 +505,16 @@
         more = pltpu.make_async_copy(tiles_in.at[unit, 3], tiles_in.at[unit, 3], tile_send.at[unit])
         sent.wait()
         pl.when(me % 2 != unit // 2)(more.wait)
+
+    for m in range(2):
+        for k in range(1, n_block):
+            last_copy(k, m).wait_recv()
+    mixed = combine(tiles.at[3, last_tile(me)], last_in)
+    window_out[me % 2 * 2] = (mixed * jnp.where(me > 0, 1.0, 0.0)).astype(bf16)
+    decode(
+        n_block, n_patch, seam, window_out, halo_out, meta_in.at[0, pl.ds(16, 8)], out, k0, k1, k2, k4,
+        place_rows, place_halo, weave, res,
+    )
 
 
 def render(order, seam, x, w_in, w_mid, w_feat, w_dens, w_conv, w_color, n_block, n_patch):

time: 24.4 us -> 24.3 us (level)
  no operation moved by 1% of the time
where the time goes in v12:
time: 24.3 us; the launch traced here: 24 us
  Pallas kernels  22.7 us (93%)
  between operations  0.66 us (3%)
  local copies, waits for them, and re-layouts  0.62 us (3%)
    pallas_call x1, Pallas kernels, render(): pl.pallas_call(functools.partial(field_kernel, n_block, n_patch), out_sha...  22.7 us
    unnamed x1, local copies, waits for them, and re-layouts  0.62 us

profile of v12, /device:TPU:225, one launch (start us, length us, event | category | flops | bytes accessed | tf_op | source)
XLA Modules:
  0.0 24.0 jit_solution(2345034979237342557)
XLA Ops:
  0.7 22.7 %field.1 = f32[3,16,256]{2,1,0:T(8,128)S(1)} custom-call(s32[1]{0:T(128)S(6)} %copy.12.seam, s32[1,16]{1,0:T(1,128)} %order_far.1, bf16[2,16,128,128]{3,2,1,0:T(8,128)(2,1)} %bitcast.2, bf16[2,32,256]{2,1,0:T(8,128)(2,1)} %w_in_far.1, bf16[2,2,256,256]{3,2,1,0:T(8,128)(2,1)} %w_mid_far.1, bf16[2,64,256]{2,1,0:T(8,128)(2,1)} %bitcast.3, ...), custom_call_target="tpu_custom_call" | custom-call | tf_op jit(solution)/shard_map/field/pallas_call | solution.py:526
  23.4 0.6 %copy.11 = f32[3,16,256]{2,1,0:T(8,128)} copy(f32[3,16,256]{2,1,0:T(8,128)S(1)} %field.1) | data formatting | bytes 98304

commit v13 on v12

--- a/solution.py
+++ b/solution.py
@@ -445,6 +445,10 @@
         return (me % 2 != unit // 2) & ((me < n_block - 1) if unit % 2 == 0 else (me > 0))
 
     for unit in range(3):
+        if unit == 2:
+            for fetch in fetches[6:]:
+                fetch.wait()
+            prepare(w_conv, w_color, k0, k1, k2, k3, k4, place_rows, place_halo, weave)
 
         @pl.when(mine(unit))
         def _():
@@ -457,9 +461,6 @@
         def _():
             window_out[1 + unit % 2] = passed[unit]
 
-    for fetch in fetches[6:]:
-        fetch.wait()
-    prepare(w_conv, w_color, k0, k1, k2, k3, k4, place_rows, place_halo, weave)
 
     for k in range(1, n_block):
         for copy in halo_copies(k):

time: 24.3 us -> 24.3 us (level)
  no operation moved by 1% of the time
where the time goes in v13:
time: 24.3 us; the launch traced here: 24 us
  Pallas kernels  22.7 us (93%)
  between operations  0.66 us (3%)
  local copies, waits for them, and re-layouts  0.62 us (3%)
    pallas_call x1, Pallas kernels, render(): pl.pallas_call(functools.partial(field_kernel, n_block, n_patch), out_sha...  22.7 us
    unnamed x1, local copies, waits for them, and re-layouts  0.62 us

profile of v13, /device:TPU:225, one launch (start us, length us, event | category | flops | bytes accessed | tf_op | source)
XLA Modules:
  0.0 24.0 jit_solution(10312521707404697974)
XLA Ops:
  0.7 22.7 %field.1 = f32[3,16,256]{2,1,0:T(8,128)S(1)} custom-call(s32[1]{0:T(128)S(6)} %copy.12.seam, s32[1,16]{1,0:T(1,128)} %order_far.1, bf16[2,16,128,128]{3,2,1,0:T(8,128)(2,1)} %bitcast.2, bf16[2,32,256]{2,1,0:T(8,128)(2,1)} %w_in_far.1, bf16[2,2,256,256]{3,2,1,0:T(8,128)(2,1)} %w_mid_far.1, bf16[2,64,256]{2,1,0:T(8,128)(2,1)} %bitcast.3, ...), custom_call_target="tpu_custom_call" | custom-call | tf_op jit(solution)/shard_map/field/pallas_call | solution.py:527
  23.4 0.6 %copy.11 = f32[3,16,256]{2,1,0:T(8,128)} copy(f32[3,16,256]{2,1,0:T(8,128)S(1)} %field.1) | data formatting | bytes 98304
